TPU v7x, 128 devices: a whole 4x4x4 slice. The times are simulated.
128 devices in a mesh: ep: 32 (over y, x, core), dp: 4 (over z).
Axes of the slice: x: 4, y: 4, z: 4, core: 2. Of those that a mesh axis runs over, the one named last changes fastest.
Arguments:
- resid: bfloat16 [2048, 4096], P(('ep', 'dp')), may hold values from -6 to 6
- queries: bfloat16 [2048, 8192], P(('ep', 'dp')), may hold values from -4.5 to 4.5
- new_keys: bfloat16 [2048, 512], P(('ep', 'dp')), may hold values from -4.5 to 4.5
- new_values: bfloat16 [2048, 512], P(('ep', 'dp')), may hold values from -6 to 6
- cache_keys: bfloat16 [2048, 128, 512], P(('ep', 'dp')), may hold values from -4.5 to 4.5
- cache_values: bfloat16 [2048, 128, 512], P(('ep', 'dp')), may hold values from -6 to 6
- cache_len: int32 [2048], P(('ep', 'dp')), may hold values from 1 to 128
- out_proj: bfloat16 [8192, 4096], P('ep'), may hold values from -0.0625 to 0.0625
- norm_gain: float32 [4096], replicated, may hold values from 0.1 to 1.9
- router: bfloat16 [4096, 64], replicated, may hold values from -4 to 4
- expert_ids: int32 [2048, 8], P(('ep', 'dp')), may hold values from 0 to 63, all different within a row; in each aligned block of 16 rows (0 to 15, 16 to 31, ...) at most 4 rows name the same one
- gate_slab: bfloat16 [128, 4096, 384], P(('ep', 'dp')), may hold values from -0.09375 to 0.09375
- up_slab: bfloat16 [128, 4096, 384], P(('ep', 'dp')), may hold values from -0.09375 to 0.09375
- down_slab: bfloat16 [128, 384, 4096], P(('ep', 'dp')), may hold values from -0.21875 to 0.21875
Outputs:
- mixed: float32 [2048, 4096], P(('ep', 'dp'))
Inputs may be any that keep to these rules, and one draw needn't show every extreme that they name: `expert_ids`: each row names 8 different experts; among the rows of one device no expert is named by more than 4 rows.
All inputs are finite; a program needn't handle non-finite values.
Results may differ from a plain program's by a relative error of at most 0.009.
Values may be sent and summed in bfloat16 or wider, within the bound.
A program may use at most 128 MiB of HBM per device.

v0:
```python
import math

import jax
import jax.numpy as jnp
from jax import lax
from jax.experimental import pallas as pl
from jax.experimental.pallas import tpu as pltpu
from jax.sharding import PartitionSpec as P

D = 4096
H = 64
KVH = 4
HD = 128
TOP = 8


def attend(queries, new_keys, new_values, cache_keys, cache_values, cache_len):
    local_rows = queries.shape[0]
    cache_span = cache_keys.shape[1]
    group_size = H // KVH
    query_heads = queries.reshape(local_rows, KVH, group_size, HD)
    past_keys = cache_keys.reshape(local_rows, cache_span, KVH, HD)
    past_values = cache_values.reshape(local_rows, cache_span, KVH, HD)
    score_scale = 1.0 / math.sqrt(HD)
    past_scores = (
        jnp.einsum("tgqd,tcgd->tgqc", query_heads, past_keys, preferred_element_type=jnp.float32)
        * score_scale
    )
    own_scores = (
        jnp.einsum(
            "tgqd,tgd->tgq",
            query_heads,
            new_keys.reshape(local_rows, KVH, HD),
            preferred_element_type=jnp.float32,
        )
        * score_scale
    )
    is_valid = lax.broadcasted_iota(jnp.int32, (local_rows, cache_span), 1) < cache_len[:, None]
    past_scores = jnp.where(is_valid[:, None, None, :], past_scores, -1e30)
    peak_score = jnp.maximum(jnp.max(past_scores, axis=3), own_scores)
    past_exp = jnp.exp(past_scores - peak_score[..., None])
    own_exp = jnp.exp(own_scores - peak_score)
    denom_sum = jnp.sum(past_exp, axis=3) + own_exp
    past_weights = (past_exp / denom_sum[..., None]).astype(jnp.bfloat16)
    own_weights = (own_exp / denom_sum).astype(jnp.bfloat16)
    blended = jnp.einsum(
        "tgqc,tcgd->tgqd", past_weights, past_values, preferred_element_type=jnp.float32
    )
    blended = blended + own_weights.astype(jnp.float32)[..., None] * new_values.reshape(
        local_rows, KVH, 1, HD
    ).astype(jnp.float32)
    return blended.reshape(local_rows, H * HD).astype(jnp.bfloat16)


MESH = pl.DeviceIdType.MESH
VMEM_LIMIT = 66_000_000


class Place:
    def __init__(self, side, depth):
        self.side, self.depth = side, depth
        ep = lax.axis_index("ep")
        self.ep = ep
        self.core = lax.rem(ep, 2)
        self.x = lax.rem(ep // 2, side)
        self.y = ep // (2 * side)
        self.z = lax.axis_index("dp")

    def at(self, dy=0, dx=0, dz=0, flip=False):
        y, x = self.line(dy, dx)
        z = lax.rem(self.z + dz, self.depth) if dz else self.z
        core = 1 - self.core if flip else self.core
        return ((y * self.side + x) * 2 + core, z)

    def line(self, dy, dx):
        return lax.rem(self.y + dy, self.side), lax.rem(self.x + dx, self.side)


def greet(devices):
    barrier = pltpu.get_barrier_semaphore()
    for device in devices:
        pl.semaphore_signal(barrier, inc=1, device_id=device, device_id_type=MESH)
    pl.semaphore_wait(barrier, len(devices))


def remote(src, dst, send, recv, device):
    return pltpu.make_async_remote_copy(
        src_ref=src, dst_ref=dst, send_sem=send, recv_sem=recv, device_id=device, device_id_type=MESH
    )


def slices_of(width, extra=0):
    step = 512
    cuts = [[start, step] for start in range(0, width, step)]
    cuts[-1][1] += extra
    return cuts


def reduce_shapes(side, depth, rows, width):
    n = width // 512
    lines = side * side
    bf, dma = jnp.bfloat16, pltpu.SemaphoreType.DMA
    tall = depth * rows
    return [
        pltpu.VMEM((side, side, tall, width), bf),
        pltpu.VMEM((side - 1, side, tall, width), bf),
        pltpu.VMEM((side, tall, width), bf),
        pltpu.VMEM((side - 1, tall, width), bf),
        pltpu.VMEM((depth, rows, width), bf),
        pltpu.VMEM((max(depth - 1, 1), rows, width), bf),
        dma((n, 2)),
        dma((n, side, side, 2)),
        dma((n, side, 2)),
        dma((n, depth, 2)),
    ]


def reduce_scatter(here, rows, width, produce, finish, lags, part, scratch):
    in1, in2, sum2, in3, sum3, in4, sem1, sem2, sem3, sem4 = scratch
    side, depth = here.side, here.depth
    cuts = slices_of(width)
    sends = []

    def core_copy(s):
        start, size = cuts[s]
        cols = pl.ds(start, size)
        return remote(
            part.at[:, :, 1 - here.core, :, cols],
            in1.at[:, :, :, cols],
            sem1.at[s, 0],
            sem1.at[s, 1],
            here.at(flip=True),
        )

    def offsets(s, a, b):
        return (a, b) if s % 2 == 0 else (b, a)

    def first_copy(s, ja, kb, sending):
        cols = pl.ds(*cuts[s])
        slot = side - ja - 1
        y, x = here.line(*offsets(s, ja, kb))
        return remote(
            in1.at[y, x, :, cols],
            in2.at[slot, kb, :, cols],
            sem2.at[s, ja, kb, 0],
            sem2.at[s, side - ja if sending else ja, kb, 1],
            here.at(*offsets(s, ja, 0)),
        )

    def second_copy(s, kb, sending):
        cols = pl.ds(*cuts[s])
        return remote(
            sum2.at[kb, :, cols],
            in3.at[side - kb - 1, :, cols],
            sem3.at[s, kb, 0],
            sem3.at[s, side - kb if sending else kb, 1],
            here.at(*offsets(s, 0, kb)),
        )

    def depth_copy(s, jz, sending):
        cols = pl.ds(*cuts[s])
        return remote(
            sum3.at[lax.rem(here.z + jz, depth), :, cols],
            in4.at[depth - jz - 1, :, cols],
            sem4.at[s, jz, 0],
            sem4.at[s, depth - jz if sending else jz, 1],
            here.at(0, 0, jz),
        )

    def go(copy):
        copy.start()
        sends.append(copy)

    def wide(value):
        return value.astype(jnp.float32)

    def phase0(s):
        cols = pl.ds(*cuts[s])
        value = produce(s, cols)
        part[:, :, :, :, cols] = value.astype(jnp.bfloat16).reshape(
            side, side, 2, depth * rows, cuts[s][1]
        )
        go(core_copy(s))

    def phase1(s):
        cols = pl.ds(*cuts[s])
        core_copy(s).wait_recv()
        for a in list(range(1, side)) + [0]:
            for b in list(range(1, side)) + [0]:
                y, x = here.line(*offsets(s, a, b))
                total = wide(part[y, x, here.core, :, cols]) + wide(in1[y, x, :, cols])
                in1[y, x, :, cols] = total.astype(jnp.bfloat16)
                if a:
                    go(first_copy(s, a, b, True))

    def phase2(s):
        cols = pl.ds(*cuts[s])
        for b in list(range(1, side)) + [0]:
            y, x = here.line(*offsets(s, 0, b))
            total = wide(in1[y, x, :, cols])
            for a in range(1, side):
                first_copy(s, a, b, False).wait_recv()
                total = total + wide(in2[a - 1, b, :, cols])
            sum2[b, :, cols] = total.astype(jnp.bfloat16)
            if b:
                go(second_copy(s, b, True))

    def phase3(s):
        cols = pl.ds(*cuts[s])
        total = wide(sum2[0, :, cols])
        for b in range(1, side):
            second_copy(s, b, False).wait_recv()
            total = total + wide(in3[b - 1, :, cols])
        if depth == 1:
            finish(s, cols, total)
            return
        sum3[:, :, cols] = total.astype(jnp.bfloat16).reshape(depth, rows, cuts[s][1])
        for jz in range(1, depth):
            go(depth_copy(s, jz, True))

    def phase4(s):
        if depth == 1:
            return
        cols = pl.ds(*cuts[s])
        total = wide(sum3[here.z, :, cols])
        for jz in range(1, depth):
            depth_copy(s, jz, False).wait_recv()
            total = total + wide(in4[jz - 1, :, cols])
        finish(s, cols, total)

    phases = tuple(zip((phase0, phase1, phase2, phase3, phase4), lags))
    for step in range(len(cuts) + phases[-1][1]):
        for phase, lag in phases:
            if 0 <= step - lag < len(cuts):
                phase(step - lag)
    for copy in sends:
        copy.wait_send()


def plane_of(here):
    side = here.side
    return (
        [here.at(flip=True)]
        + [here.at(dy=j) for j in range(1, side)]
        + [here.at(dx=j) for j in range(1, side)]
    )


def projection_kernel(
    side, attended, weight_hbm, resid, gain, router, chosen, hidden, packed, weight, regrouped, part, wsem, ssem, rsem, *scratch
):
    here = Place(side, 1)
    rows = attended.shape[0]
    count = 2 * side * side
    width = attended.shape[1] // count
    z = lax.axis_index("dp")
    load = pltpu.make_async_copy(weight_hbm, weight, wsem)
    load.start()

    def peer(j):
        return lax.rem(here.ep + j, count)

    greet([(peer(j), z) for j in range(1, count)])

    def piece(index):
        return attended.at[:, pl.ds(pl.multiple_of(index * width, 128), width)]

    def exchange(j, sending):
        return remote(
            piece(peer(j)),
            regrouped.at[here.ep],
            ssem.at[j],
            rsem.at[count - j if sending else j],
            (peer(j), z),
        )

    for j in range(1, count):
        exchange(j, True).start()
    regrouped[here.ep] = attended[:, pl.ds(pl.multiple_of(here.ep * width, 128), width)]
    load.wait()
    for j in range(1, count):
        remote(
            piece(peer(j)), regrouped.at[peer(j)], ssem.at[j], rsem.at[j], (peer(j), z)
        ).wait_recv()

    def produce(s, cols):
        left = regrouped[...].reshape(count * rows, width)
        return jnp.dot(left, weight[:, cols], preferred_element_type=jnp.float32)

    def finish(s, cols, total):
        value = resid[:, cols].astype(jnp.float32) + total
        hidden[:, cols] = value
        squares.append(jnp.sum(value * value, axis=1, keepdims=True))

    squares = []

    reduce_scatter(here, rows, hidden.shape[1], produce, finish, (0, 2, 5, 8, 8), part, scratch)
    features = hidden.shape[1]
    scale = lax.rsqrt(jnp.maximum(sum(squares) / features, 0.25))
    logits = jnp.zeros((rows, router.shape[1]), jnp.float32)
    for start, size in slices_of(features):
        cols = pl.ds(start, size)
        normed = (hidden[:, cols] * scale * gain[:, cols]).astype(jnp.bfloat16)
        packed[:, cols] = normed
        logits = logits + jnp.dot(normed, router[cols, :], preferred_element_type=jnp.float32)
    named = chosen[...] > 0
    peak = jnp.max(jnp.where(named, logits, -jnp.inf), axis=1, keepdims=True)
    grown = jnp.where(named, jnp.exp(jnp.where(named, logits - peak, 0.0)), 0.0)
    probs = grown / jnp.sum(grown, axis=1, keepdims=True)
    packed[:, features:] = jnp.zeros((rows, packed.shape[1] - features), jnp.bfloat16)
    packed[:, features : features + router.shape[1]] = probs.astype(jnp.bfloat16)
    for j in range(1, count):
        exchange(j, True).wait_send()


def project(side, attended, out_proj, resid, gain, router, chosen):
    rows, width = resid.shape
    count = 2 * side * side
    dma = pltpu.SemaphoreType.DMA
    vmem = pl.BlockSpec(memory_space=pltpu.VMEM)
    return pl.pallas_call(
        lambda *refs: projection_kernel(side, *refs),
        out_shape=(
            jax.ShapeDtypeStruct((rows, width), jnp.float32),
            jax.ShapeDtypeStruct((rows, width + pl.cdiv(router.shape[1], 128) * 128), jnp.bfloat16),
        ),
        in_specs=[vmem, pl.BlockSpec(memory_space=pl.ANY), vmem, vmem, vmem, vmem],
        out_specs=(vmem, vmem),
        scratch_shapes=[
            pltpu.VMEM(out_proj.shape, jnp.bfloat16),
            pltpu.VMEM((count, rows, attended.shape[1] // count), jnp.bfloat16),
            pltpu.VMEM((side, side, 2, rows, width), jnp.bfloat16),
            dma(()),
            dma((count,)),
            dma((count,)),
        ]
        + reduce_shapes(side, 1, rows, width),
        compiler_params=pltpu.CompilerParams(
            collective_id=0, has_side_effects=True, vmem_limit_bytes=VMEM_LIMIT
        ),
    )(attended, out_proj, resid, gain, router, chosen)


def all_gather(here, own, held, consume, zsem, lsem, csem, send_sem, copy_sem):
    side, depth = here.side, here.depth
    width = D
    cuts = slices_of(width, own.shape[1] - width)
    sends = []
    rows = own.shape[0]

    def rows_of(z):
        return pl.ds(pl.multiple_of(z * rows, rows), rows)

    local_copy = pltpu.make_async_copy(own, held.at[here.y, here.x, here.core, rows_of(here.z)], copy_sem)
    local_copy.start()

    def go(copy):
        copy.start()
        sends.append(copy)

    def depth_copy(s, j, sending):
        cols = pl.ds(*cuts[s])
        z = here.z if sending else lax.rem(here.z + j, depth)
        return remote(
            own.at[:, cols],
            held.at[here.y, here.x, here.core, rows_of(z), cols],
            zsem.at[s, j, 0],
            zsem.at[s, depth - j if sending else j, 1],
            here.at(0, 0, j),
        )

    def line_ref(s, ky, kx, core):
        y, x = here.line(ky, kx)
        return held.at[y, x, core, :, pl.ds(*cuts[s])]

    def plane_send(s, ky, kx, jy, jx):
        ref = line_ref(s, ky, kx, here.core)
        go(
            remote(
                ref,
                ref,
                send_sem.at[s, ky, kx, jy, jx],
                lsem.at[s, (ky - jy) % side, (kx - jx) % side],
                here.at(jy, jx),
            )
        )

    def core_send(s, ky, kx):
        ref = line_ref(s, ky, kx, here.core)
        go(remote(ref, ref, csem.at[s, ky, kx, 0], csem.at[s, ky, kx, 1], here.at(flip=True)))

    def plane_wait(s, ky, kx):
        ref = line_ref(s, ky, kx, here.core)
        remote(ref, ref, send_sem.at[s, 0, 0, 0, 0], lsem.at[s, ky, kx], here.at(flip=True)).wait_recv()

    def core_wait(s, ky, kx):
        ref = line_ref(s, ky, kx, 1 - here.core)
        remote(ref, ref, csem.at[s, ky, kx, 0], csem.at[s, ky, kx, 1], here.at(flip=True)).wait_recv()

    def turn(s, a, b):
        return (a, b) if s % 2 == 0 else (b, a)

    def phase1(s):
        for j in range(1, depth):
            depth_copy(s, j, False).wait_recv()
        for j in range(1, side):
            plane_send(s, 0, 0, *turn(s, j, 0))
            plane_send(s, 0, 0, *turn(s, 0, j))
        core_send(s, 0, 0)

    def phase2(s):
        for k in range(1, side):
            plane_wait(s, *turn(s, k, 0))
            for j in range(1, side):
                plane_send(s, *turn(s, k, 0), *turn(s, 0, j))
            core_send(s, *turn(s, k, 0))

    def phase3(s):
        for b in range(1, side):
            for a in range(side):
                plane_wait(s, *turn(s, a, b))
                core_send(s, *turn(s, a, b))

    def phase0(s):
        for j in range(1, depth):
            go(depth_copy(s, j, True))

    local_copy.wait()
    def phase4(s):
        for a in range(side):
            for b in range(side):
                core_wait(s, a, b)
        consume(s)

    phases = ((phase0, 0), (phase1, 2), (phase2, 4), (phase3, 6), (phase4, 7))
    for step in range(len(cuts) + phases[-1][1]):
        for phase, lag in phases:
            if 0 <= step - lag < len(cuts):
                phase(step - lag)
    for copy in sends:
        copy.wait_send()


def expert_kernel(
    side, depth, own, gate_hbm, up_hbm, down_hbm, mixed,
    gate, up, down, held, act, gate_sum, up_sum, wsem, zsem, lsem, csem, send_sem, copy_sem, *scratch
):
    here = Place(side, depth)
    rows = own.shape[0]
    loads = [
        pltpu.make_async_copy(src.at[0], dst, wsem.at[i])
        for i, (src, dst) in enumerate(((gate_hbm, gate), (up_hbm, up), (down_hbm, down)))
    ]
    for load in loads:
        load.start()
    greet(plane_of(here) + [here.at(0, 0, j) for j in range(1, depth)])
    group = side * 2 * depth * rows

    def rows_at(y):
        return pl.ds(pl.multiple_of(y * group, group), group)

    def consume(s):
        if s == 0:
            loads[0].wait()
            loads[1].wait()
        start = 512 * s

        def step(y, carry):
            block = held[y, :, :, :, start : start + 512].reshape(group, 512)
            for weight, total in ((gate, gate_sum), (up, up_sum)):
                value = jnp.dot(
                    block, weight[start : start + 512, :], preferred_element_type=jnp.float32
                )
                total[rows_at(y), :] = value if s == 0 else total[rows_at(y), :] + value
            return carry

        lax.fori_loop(0, side, step, 0)

    all_gather(here, own, held, consume, zsem, lsem, csem, send_sem, copy_sem)
    loads[2].wait()
    expert = (here.ep * depth + here.z) // 2

    def activate(y, carry):
        tail = held[y, :, :, :, D:].reshape(group, held.shape[-1] - D)
        lane = lax.broadcasted_iota(jnp.int32, tail.shape, 1)
        weight = jnp.sum(
            jnp.where(lane == expert, tail.astype(jnp.float32), 0.0), axis=1, keepdims=True
        )
        gate_val = gate_sum[rows_at(y), :]
        value = gate_val / (1.0 + jnp.exp(-gate_val)) * up_sum[rows_at(y), :] * weight
        act[rows_at(y), :] = value.astype(jnp.bfloat16)
        return carry

    lax.fori_loop(0, side, activate, 0)

    def produce(s, cols):
        return jnp.dot(act[...], down[:, cols], preferred_element_type=jnp.float32)

    def finish(s, cols, total):
        mixed[:, cols] = total

    reduce_scatter(here, rows, mixed.shape[1], produce, finish, (0, 1, 3, 5, 7), held, scratch)


def run_experts(side, depth, packed, gate_slab, up_slab, down_slab):
    rows, width = packed.shape[0], down_slab.shape[2]
    n = width // 512
    dma = pltpu.SemaphoreType.DMA
    count = 2 * side * side * depth
    vmem, anywhere = pl.BlockSpec(memory_space=pltpu.VMEM), pl.BlockSpec(memory_space=pl.ANY)
    return pl.pallas_call(
        lambda *refs: expert_kernel(side, depth, *refs),
        out_shape=jax.ShapeDtypeStruct((rows, width), jnp.float32),
        in_specs=[vmem, anywhere, anywhere, anywhere],
        out_specs=vmem,
        scratch_shapes=[
            pltpu.VMEM(gate_slab.shape[1:], jnp.bfloat16),
            pltpu.VMEM(up_slab.shape[1:], jnp.bfloat16),
            pltpu.VMEM(down_slab.shape[1:], jnp.bfloat16),
            pltpu.VMEM((side, side, 2, depth * rows, packed.shape[1]), jnp.bfloat16),
            pltpu.VMEM((count * rows, gate_slab.shape[2]), jnp.bfloat16),
            pltpu.VMEM((count * rows, gate_slab.shape[2]), jnp.float32),
            pltpu.VMEM((count * rows, gate_slab.shape[2]), jnp.float32),
            dma((3,)),
            dma((n, depth, 2)),
            dma((n, side, side)),
            dma((n, side, side, 2)),
            dma((n, side, side, side, side)),
            dma(()),
        ]
        + reduce_shapes(side, depth, rows, width),
        compiler_params=pltpu.CompilerParams(
            collective_id=1, has_side_effects=True, vmem_limit_bytes=VMEM_LIMIT
        ),
    )(packed, gate_slab, up_slab, down_slab)


def local(
    resid,
    queries,
    new_keys,
    new_values,
    cache_keys,
    cache_values,
    cache_len,
    out_proj,
    norm_gain,
    router,
    expert_ids,
    gate_slab,
    up_slab,
    down_slab,
):
    attended = attend(queries, new_keys, new_values, cache_keys, cache_values, cache_len)
    side = math.isqrt(lax.axis_size("ep") // 2)
    depth = lax.axis_size("dp")
    labels = jnp.arange(router.shape[1], dtype=jnp.int32)
    chosen = jnp.any(expert_ids[:, :, None] == labels[None, None, :], axis=1).astype(jnp.float32)
    hidden, packed = project(
        side, attended, out_proj, resid, norm_gain.reshape(1, -1), router, chosen
    )
    return hidden + run_experts(side, depth, packed, gate_slab, up_slab, down_slab)


def solution(mesh):
    in_specs = (
        P(("ep", "dp"), None),
        P(("ep", "dp"), None),
        P(("ep", "dp"), None),
        P(("ep", "dp"), None),
        P(("ep", "dp"), None, None),
        P(("ep", "dp"), None, None),
        P(("ep", "dp")),
        P("ep", None),
        P(),
        P(),
        P(("ep", "dp"), None),
        P(("ep", "dp"), None, None),
        P(("ep", "dp"), None, None),
        P(("ep", "dp"), None, None),
    )
    out_specs = P(("ep", "dp"), None)
    return jax.shard_map(local, mesh=mesh, in_specs=in_specs, out_specs=out_specs, check_vma=False)
```

profile of v0, /device:TPU:0, one launch (start us, length us, event | category | flops | bytes accessed | tf_op | source)
XLA Modules:
  0.0 224.4 jit_solution(18363933769974475060)
XLA Ops:
  0.0 0.7 iota_compare_fusion.1
  0.7 0.8 copy.21
  1.5 0.1 fusion.21
  1.6 0.6 convert_element_type.35.refs_5_
  2.2 0.7 reshape.55
  2.9 0.7 reshape.51
  3.7 1.0 copy.27
  4.7 0.0 copy-start.2
  4.7 0.2 fusion.25
  4.9 3.0 %fusion.24 = (f32[16,4,16]{2,1,0:T(4,128)S(1)}, f32[16,4,16,128]{3,2,1,0:T(8,128)S(1)}) fusion(bf16[16,4,16,128]{3,2,1,0:T(8,128)(2,1)S(1)} %bitcast.39, pred[16,128]{1,0:T(8,128)(4,1)S(1)} %iota_compare_fusion.1, bf16[16,128,512]{2,1,0:T(8,128)(2,1)} %param.18), kind=kOutput, calls=%fused_computation.24 | convolution fusion | flops 33946624 | bytes 2889728 | tf_op jit(solution)/shard_map/tgqd,tcgd->tgqc/dot_general | solution.py:26
  8.0 0.4 fusion.18
  8.5 0.0 copy-done.2
  8.5 0.0 copy-start
  8.5 0.8 fusion.15
  9.2 0.9 copy.48
  10.1 0.0 copy-done
  10.1 1.3 copy.22.refs_4_
  11.5 39.4 %shard_map.136 = (f32[16,4096]{1,0:T(8,128)}, bf16[16,4224]{1,0:T(8,128)(2,1)}) custom-call(bf16[16,8192]{1,0:T(8,128)(2,1)} %bitcast.40, bf16[256,4096]{1,0:T(8,128)(2,1)} %refs_1_.2, bf16[16,4096]{1,0:T(8,128)(2,1)} %refs_2_.2, f32[1,4096]{1,0:T(1,128)} %bitcast.45, bf16[4096,64]{1,0:T(8,128)(2,1)} %copy.22.refs_4_, f32[16,64]{1,0:T(8,128)} %convert_element_type.35.refs_5_), custom_call_target="tpu_custom_call" | custom-call | tf_op jit(solution)/shard_map/pallas_call | solution.py:321
  50.9 0.0 copy-start.1
  50.9 171.7 %shard_map.137 = f32[16,4096]{1,0:T(8,128)} custom-call(bf16[16,4224]{1,0:T(8,128)(2,1)} %get-tuple-element.8.refs_0_, bf16[1,4096,384]{2,1,0:T(8,128)(2,1)} %refs_1_.3, bf16[1,4096,384]{2,1,0:T(8,128)(2,1)} %refs_2_.3, bf16[1,384,4096]{2,1,0:T(8,128)(2,1)} %refs_3_.1), custom_call_target="tpu_custom_call" | custom-call | tf_op jit(solution)/shard_map/pallas_call | solution.py:511
  222.7 0.0 copy-done.1
  222.7 1.7 add.11
  (2 shorter events, 0.1 us)
Async XLA Ops:
  4.7 3.8 %copy-start.2 = (bf16[16,128,512]{2,1,0:T(8,128)(2,1)S(1)}, bf16[16,128,512]{2,1,0:T(8,128)(2,1)}, u32[]{:S(2)}) copy-start(bf16[16,128,512]{2,1,0:T(8,128)(2,1)} %param.19) | copy-start | bytes 6291460
  8.5 1.6 copy-start
  50.9 171.8 %copy-start.1 = (f32[16,4096]{1,0:T(8,128)S(1)}, f32[16,4096]{1,0:T(8,128)}, u32[]{:S(2)}) copy-start(f32[16,4096]{1,0:T(8,128)} %get-tuple-element.7) | copy-start | bytes 786436
where the time goes:
time: 225 us; the launch traced here: 224 us
  Pallas kernels  211 us (94%)
  local copies, waits for them, and re-layouts  5.45 us (2%)
  matrix products  4.03 us (2%)
  other arithmetic  3.6 us (2%)
    pallas_call x1, Pallas kernels, run_experts(): pl.pallas_call(lambda *refs: expert_kernel(side, depth, *refs), out_shape...  172 us
    pallas_call x1, Pallas kernels, project(): pl.pallas_call(lambda *refs: projection_kernel(side, *refs), out_shape=(j...  39.4 us

commit v1 on v0

--- a/solution.py
+++ b/solution.py
@@ -341,194 +341,367 @@
     )(attended, out_proj, resid, gain, router, chosen)
 
 
-def all_gather(here, own, held, consume, zsem, lsem, csem, send_sem, copy_sem):
-    side, depth = here.side, here.depth
-    width = D
-    cuts = slices_of(width, own.shape[1] - width)
+AXES = ("y", "x", "z")
+ORDERS = (
+    ("y", "x", "z"),
+    ("z", "x", "y"),
+    ("y", "z", "x"),
+    ("y", "x", "z"),
+    ("z", "x", "y"),
+    ("y", "z", "x"),
+    ("y", "x", "z"),
+    ("z", "x", "y"),
+)
+STEP = 512
+HALF = 256
+
+
+class Spot:
+    def __init__(self):
+        ep = lax.axis_index("ep")
+        self.core = lax.rem(ep, 2)
+        self.pos = {"x": lax.rem(ep // 2, 4), "y": ep // 8, "z": lax.axis_index("dp")}
+
+    def coord(self, axis, off):
+        return lax.rem(self.pos[axis] + off, 4) if off else self.pos[axis]
+
+    def at(self, axis=None, off=0, flip=False):
+        place = dict(self.pos)
+        if axis:
+            place[axis] = self.coord(axis, off)
+        core = 1 - self.core if flip else self.core
+        return ((place["y"] * 4 + place["x"]) * 2 + core, place["z"])
+
+    def index(self, fixed):
+        return tuple(fixed.get(axis, slice(None)) for axis in AXES)
+
+
+def expert_kernel(own, gate_hbm, up_hbm, down_hbm, mixed, *scratch):
+    n = len(ORDERS)
+    gu, down, act, total, wsem, nsem, fsem, csem, rnear, rfar, rcore = scratch[:11]
+    scratch = scratch[11:]
+    held, inner = scratch[:n], scratch[n : 2 * n]
+    nears = [scratch[2 * n + 3 * s : 2 * n + 3 * s + 3] for s in range(n)]
+    fars = [scratch[5 * n + 3 * s : 5 * n + 3 * s + 3] for s in range(n)]
+    here = Spot()
+    rows = own.shape[0]
+    hidden = act.shape[1]
+    loads = [
+        pltpu.make_async_copy(gate_hbm.at[0], gu.at[:, pl.ds(0, hidden)], wsem.at[0]),
+        pltpu.make_async_copy(up_hbm.at[0], gu.at[:, pl.ds(hidden, hidden)], wsem.at[1]),
+        pltpu.make_async_copy(down_hbm.at[0], down, wsem.at[2]),
+    ]
+    for load in loads:
+        load.start()
+    greet([here.at(flip=True)] + [here.at(axis, off) for axis in AXES for off in (1, 2, 3)])
     sends = []
-    rows = own.shape[0]
-
-    def rows_of(z):
-        return pl.ds(pl.multiple_of(z * rows, rows), rows)
-
-    local_copy = pltpu.make_async_copy(own, held.at[here.y, here.x, here.core, rows_of(here.z)], copy_sem)
-    local_copy.start()
 
     def go(copy):
         copy.start()
         sends.append(copy)
 
-    def depth_copy(s, j, sending):
-        cols = pl.ds(*cuts[s])
-        z = here.z if sending else lax.rem(here.z + j, depth)
-        return remote(
-            own.at[:, cols],
-            held.at[here.y, here.x, here.core, rows_of(z), cols],
-            zsem.at[s, j, 0],
-            zsem.at[s, depth - j if sending else j, 1],
-            here.at(0, 0, j),
-        )
-
-    def line_ref(s, ky, kx, core):
-        y, x = here.line(ky, kx)
-        return held.at[y, x, core, :, pl.ds(*cuts[s])]
-
-    def plane_send(s, ky, kx, jy, jx):
-        ref = line_ref(s, ky, kx, here.core)
-        go(
-            remote(
-                ref,
-                ref,
-                send_sem.at[s, ky, kx, jy, jx],
-                lsem.at[s, (ky - jy) % side, (kx - jx) % side],
-                here.at(jy, jx),
-            )
-        )
-
-    def core_send(s, ky, kx):
-        ref = line_ref(s, ky, kx, here.core)
-        go(remote(ref, ref, csem.at[s, ky, kx, 0], csem.at[s, ky, kx, 1], here.at(flip=True)))
-
-    def plane_wait(s, ky, kx):
-        ref = line_ref(s, ky, kx, here.core)
-        remote(ref, ref, send_sem.at[s, 0, 0, 0, 0], lsem.at[s, ky, kx], here.at(flip=True)).wait_recv()
-
-    def core_wait(s, ky, kx):
-        ref = line_ref(s, ky, kx, 1 - here.core)
-        remote(ref, ref, csem.at[s, ky, kx, 0], csem.at[s, ky, kx, 1], here.at(flip=True)).wait_recv()
-
-    def turn(s, a, b):
-        return (a, b) if s % 2 == 0 else (b, a)
-
-    def phase1(s):
-        for j in range(1, depth):
-            depth_copy(s, j, False).wait_recv()
-        for j in range(1, side):
-            plane_send(s, 0, 0, *turn(s, j, 0))
-            plane_send(s, 0, 0, *turn(s, 0, j))
-        core_send(s, 0, 0)
-
-    def phase2(s):
-        for k in range(1, side):
-            plane_wait(s, *turn(s, k, 0))
-            for j in range(1, side):
-                plane_send(s, *turn(s, k, 0), *turn(s, 0, j))
-            core_send(s, *turn(s, k, 0))
-
-    def phase3(s):
-        for b in range(1, side):
-            for a in range(side):
-                plane_wait(s, *turn(s, a, b))
-                core_send(s, *turn(s, a, b))
-
-    def phase0(s):
-        for j in range(1, depth):
-            go(depth_copy(s, j, True))
-
-    local_copy.wait()
-    def phase4(s):
-        for a in range(side):
-            for b in range(side):
-                core_wait(s, a, b)
-        consume(s)
-
-    phases = ((phase0, 0), (phase1, 2), (phase2, 4), (phase3, 6), (phase4, 7))
-    for step in range(len(cuts) + phases[-1][1]):
-        for phase, lag in phases:
-            if 0 <= step - lag < len(cuts):
-                phase(step - lag)
-    for copy in sends:
-        copy.wait_send()
-
-
-def expert_kernel(
-    side, depth, own, gate_hbm, up_hbm, down_hbm, mixed,
-    gate, up, down, held, act, gate_sum, up_sum, wsem, zsem, lsem, csem, send_sem, copy_sem, *scratch
-):
-    here = Place(side, depth)
-    rows = own.shape[0]
-    loads = [
-        pltpu.make_async_copy(src.at[0], dst, wsem.at[i])
-        for i, (src, dst) in enumerate(((gate_hbm, gate), (up_hbm, up), (down_hbm, down)))
-    ]
-    for load in loads:
-        load.start()
-    greet(plane_of(here) + [here.at(0, 0, j) for j in range(1, depth)])
-    group = side * 2 * depth * rows
-
-    def rows_at(y):
-        return pl.ds(pl.multiple_of(y * group, group), group)
+    def cols_of(s):
+        return pl.ds(STEP * s, held[s].shape[-1])
+
+    def halves(s, d, width):
+        return (slice(None),) * 1 + (pl.ds(0, HALF) if d == 0 else pl.ds(HALF, width - HALF),)
+
+    def spread_index(s, p, off, core=None):
+        order = ORDERS[s]
+        fixed = {axis: here.pos[axis] for axis in order[p + 1 :]}
+        fixed[order[p]] = here.coord(order[p], off)
+        return (here.core if core is None else core,) + here.index(fixed)
+
+    def spread(s, p, off, core=None):
+        return held[s].at[spread_index(s, p, off, core)]
+
+    def spread_half(s, p, off, d):
+        width = held[s].shape[-1]
+        return held[s].at[spread_index(s, p, off) + halves(s, d, width)]
+
+    def direct_gather(s, p):
+        return p == 0 or (p == 1 and s < 3)
+
+    def gather_near(s, p):
+        axis = ORDERS[s][p]
+        for d, off in enumerate((1, 3)):
+            src = own.at[:, cols_of(s)] if p == 0 else spread(s, p, 0)
+            go(remote(src, spread(s, p, 0), nsem.at[s, p, d, 0], nsem.at[s, p, d, 1], here.at(axis, off)))
+        if direct_gather(s, p):
+            src = own.at[:, cols_of(s)] if p == 0 else spread(s, p, 0)
+            go(remote(src, spread(s, p, 0), fsem.at[s, p, 0, 0], fsem.at[s, p, 0, 1], here.at(axis, 2)))
+        if p == 2:
+            give(s, 0, 0)
+
+    def gather_far(s, p):
+        axis = ORDERS[s][p]
+        for d, (off, back) in enumerate(((1, 3), (3, 1))):
+            ref = spread(s, p, back)
+            remote(ref, ref, nsem.at[s, p, d, 0], nsem.at[s, p, d, 1], here.at(axis, back)).wait_recv()
+            if not direct_gather(s, p):
+                ref = spread_half(s, p, back, d)
+                go(remote(ref, ref, fsem.at[s, p, d, 0], fsem.at[s, p, d, 1], here.at(axis, off)))
+            if p == 2:
+                give(s, 1 + d, back)
+
+    def gather_end(s, p):
+        axis = ORDERS[s][p]
+        if direct_gather(s, p):
+            ref = spread(s, p, 2)
+            remote(ref, ref, fsem.at[s, p, 0, 0], fsem.at[s, p, 0, 1], here.at(axis, 2)).wait_recv()
+        else:
+            for d, back in enumerate((3, 1)):
+                ref = spread_half(s, p, 2, d)
+                remote(ref, ref, fsem.at[s, p, d, 0], fsem.at[s, p, d, 1], here.at(axis, back)).wait_recv()
+        if p == 2:
+            give(s, 3, 2)
+
+    def give(s, k, off):
+        ref = spread(s, 2, off)
+        go(remote(ref, ref, csem.at[s, k, 0], csem.at[s, k, 1], here.at(flip=True)))
+
+    def take(s):
+        for k, off in enumerate((0, 3, 1, 2)):
+            ref = spread(s, 2, off, 1 - here.core)
+            remote(ref, ref, csem.at[s, k, 0], csem.at[s, k, 1], here.at(flip=True)).wait_recv()
+
+    group = 32 * rows
+
+    def rows_at(i):
+        return pl.ds(pl.multiple_of(i * group, group), group)
 
     def consume(s):
         if s == 0:
             loads[0].wait()
             loads[1].wait()
-        start = 512 * s
-
-        def step(y, carry):
-            block = held[y, :, :, :, start : start + 512].reshape(group, 512)
-            for weight, total in ((gate, gate_sum), (up, up_sum)):
+
+        def step(i, carry):
+            block = held[s][i // 2, pl.ds(2 * lax.rem(i, 2), 2), :, :, :, :STEP].reshape(group, STEP)
+            value = jnp.dot(block, gu[STEP * s : STEP * s + STEP, :], preferred_element_type=jnp.float32)
+            total[rows_at(i), :] = value if s == 0 else total[rows_at(i), :] + value
+            return carry
+
+        lax.fori_loop(0, 4, step, 0)
+
+    def start(s):
+        held[s][here.core, here.pos["y"], here.pos["x"], here.pos["z"]] = own[:, cols_of(s)]
+        gather_near(s, 0)
+
+    def second(s):
+        gather_far(s, 0)
+        gather_end(s, 0)
+        gather_near(s, 1)
+
+    def third(s):
+        gather_far(s, 1)
+
+    def fourth(s):
+        gather_end(s, 1)
+        gather_near(s, 2)
+
+    def fifth(s):
+        gather_far(s, 2)
+
+    def sixth(s):
+        gather_end(s, 2)
+        take(s)
+        consume(s)
+
+    groups = ((0, 1, 2), (3, 4, 5), (6, 7))
+    plan = (
+        (start, 0), (start, 1), (start, 2),
+        (second, 0), (second, 1), (third, 0), (second, 2), (fourth, 0),
+        (third, 1), (fourth, 1), (third, 2), (fifth, 0), (fourth, 2),
+        (sixth, 0), (fifth, 1), (sixth, 1), (fifth, 2), (sixth, 2),
+    )
+    for phase, g in plan:
+        for s in groups[g]:
+            phase(s)
+    for copy in sends:
+        copy.wait_send()
+    sends.clear()
+    loads[2].wait()
+    expert = (lax.axis_index("ep") * 4 + here.pos["z"]) // 2
+
+    def activate(i, carry):
+        tail = held[n - 1][i // 2, pl.ds(2 * lax.rem(i, 2), 2), :, :, :, STEP:].reshape(group, 128)
+        lane = lax.broadcasted_iota(jnp.int32, tail.shape, 1)
+        weight = jnp.sum(jnp.where(lane == expert, tail.astype(jnp.float32), 0.0), axis=1, keepdims=True)
+        gate_val = total[rows_at(i), :hidden]
+        value = gate_val / (1.0 + jnp.exp(-gate_val)) * total[rows_at(i), hidden:] * weight
+        act[rows_at(i), :] = value.astype(jnp.bfloat16)
+        return carry
+
+    lax.fori_loop(0, 4, activate, 0)
+
+    def fold(s, p, off):
+        order = ORDERS[s][::-1]
+        fixed = {axis: here.pos[axis] for axis in order[:p]}
+        fixed[order[p]] = here.coord(order[p], off)
+        return here.index(fixed)
+
+    def direct_fold(s, p):
+        return p == 2 or (p == 1 and s >= n - 2)
+
+    def gain(s, p, off):
+        index = fold(s, p, off)
+        if p == 0:
+            mine = held[s][(here.core,) + index + (slice(None), pl.ds(0, STEP))]
+            return mine + inner[s][index]
+        return inner[s][index]
+
+    def core_copy(s):
+        return remote(
+            held[s].at[1 - here.core, :, :, :, :, pl.ds(0, STEP)],
+            inner[s],
+            rcore.at[s, 0],
+            rcore.at[s, 1],
+            here.at(flip=True),
+        )
+
+    def produce(s):
+        def step(core):
+            def one(h, carry):
+                i = 2 * core + h
                 value = jnp.dot(
-                    block, weight[start : start + 512, :], preferred_element_type=jnp.float32
+                    act[rows_at(i), :], down[:, STEP * s : STEP * s + STEP], preferred_element_type=jnp.float32
                 )
-                total[rows_at(y), :] = value if s == 0 else total[rows_at(y), :] + value
-            return carry
-
-        lax.fori_loop(0, side, step, 0)
-
-    all_gather(here, own, held, consume, zsem, lsem, csem, send_sem, copy_sem)
-    loads[2].wait()
-    expert = (here.ep * depth + here.z) // 2
-
-    def activate(y, carry):
-        tail = held[y, :, :, :, D:].reshape(group, held.shape[-1] - D)
-        lane = lax.broadcasted_iota(jnp.int32, tail.shape, 1)
-        weight = jnp.sum(
-            jnp.where(lane == expert, tail.astype(jnp.float32), 0.0), axis=1, keepdims=True
-        )
-        gate_val = gate_sum[rows_at(y), :]
-        value = gate_val / (1.0 + jnp.exp(-gate_val)) * up_sum[rows_at(y), :] * weight
-        act[rows_at(y), :] = value.astype(jnp.bfloat16)
-        return carry
-
-    lax.fori_loop(0, side, activate, 0)
-
-    def produce(s, cols):
-        return jnp.dot(act[...], down[:, cols], preferred_element_type=jnp.float32)
-
-    def finish(s, cols, total):
-        mixed[:, cols] = total
-
-    reduce_scatter(here, rows, mixed.shape[1], produce, finish, (0, 1, 3, 5, 7), held, scratch)
-
-
-def run_experts(side, depth, packed, gate_slab, up_slab, down_slab):
+                held[s][core, pl.ds(2 * h, 2), :, :, :, :STEP] = value.astype(jnp.bfloat16).reshape(
+                    2, 4, 4, rows, STEP
+                )
+                return carry
+
+            lax.fori_loop(0, 2, one, 0)
+
+        step(1 - here.core)
+        go(core_copy(s))
+        step(here.core)
+
+    def half_of(ref, index, d):
+        return ref.at[index + (slice(None), pl.ds(HALF * d, HALF))]
+
+    def lead(p):
+        return (slice(None),) * (2 - p)
+
+    def far_copy(s, p, d, sending):
+        axis = ORDERS[s][2 - p]
+        index = fold(s, p, 2)
+        if direct_fold(s, p):
+            return remote(
+                inner[s].at[index], fars[s][p], rfar.at[s, p, 0, 0], rfar.at[s, p, 0, 1], here.at(axis, 2)
+            )
+        return remote(
+            half_of(inner[s], index, d),
+            half_of(fars[s][p], lead(p), d),
+            rfar.at[s, p, d, 0],
+            rfar.at[s, p, d, 1],
+            here.at(axis, (1, 3)[d]),
+        )
+
+    def near_copy(s, p, d):
+        axis = ORDERS[s][2 - p]
+        off = (1, 3)[d]
+        return remote(
+            inner[s].at[fold(s, p, off)],
+            nears[s][p].at[d],
+            rnear.at[s, p, d, 0],
+            rnear.at[s, p, d, 1],
+            here.at(axis, off),
+        )
+
+    def fold_far(s, p):
+        if p == 0:
+            core_copy(s).wait_recv()
+            inner[s][fold(s, 0, 2)] = gain(s, 0, 2)
+        if direct_fold(s, p):
+            go(far_copy(s, p, 0, True))
+            fold_near(s, p)
+        else:
+            for d in range(2):
+                go(far_copy(s, p, d, True))
+
+    def fold_near(s, p):
+        for d, off in enumerate((1, 3)):
+            index = fold(s, p, off)
+            if direct_fold(s, p):
+                if p == 0:
+                    inner[s][index] = gain(s, p, off)
+            else:
+                far_copy(s, p, d, False).wait_recv()
+                if p == 0:
+                    inner[s][index] = gain(s, p, off)
+                part = index + (slice(None), pl.ds(HALF * d, HALF))
+                inner[s][part] = inner[s][part] + fars[s][p][lead(p) + (slice(None), pl.ds(HALF * d, HALF))]
+            go(near_copy(s, p, d))
+
+    def fold_end(s, p):
+        value = gain(s, p, 0).astype(jnp.float32)
+        for d in range(2):
+            near_copy(s, p, d).wait_recv()
+            value = value + nears[s][p][d].astype(jnp.float32)
+        if direct_fold(s, p):
+            far_copy(s, p, 0, False).wait_recv()
+            value = value + fars[s][p][...].astype(jnp.float32)
+        if p == 2:
+            mixed[:, STEP * s : STEP * s + STEP] = value
+        else:
+            inner[s][fold(s, p, 0)] = value.astype(jnp.bfloat16)
+
+    def next_fold(s, p):
+        fold_end(s, p - 1)
+        fold_far(s, p)
+
+    def middle(s):
+        if not direct_fold(s, 1):
+            fold_near(s, 1)
+
+    phases = (
+        (produce, 0),
+        (lambda s: fold_far(s, 0), 1),
+        (lambda s: fold_near(s, 0), 3),
+        (lambda s: next_fold(s, 1), 5),
+        (middle, 6),
+        (lambda s: next_fold(s, 2), 7),
+        (lambda s: fold_end(s, 2), 8),
+    )
+    for step in range(n + phases[-1][1]):
+        for phase, lag in phases:
+            if 0 <= step - lag < n:
+                phase(step - lag)
+    for copy in sends:
+        copy.wait_send()
+
+
+def run_experts(packed, gate_slab, up_slab, down_slab):
     rows, width = packed.shape[0], down_slab.shape[2]
-    n = width // 512
-    dma = pltpu.SemaphoreType.DMA
-    count = 2 * side * side * depth
+    hidden = gate_slab.shape[2]
+    n = len(ORDERS)
+    dma, bf = pltpu.SemaphoreType.DMA, jnp.bfloat16
     vmem, anywhere = pl.BlockSpec(memory_space=pltpu.VMEM), pl.BlockSpec(memory_space=pl.ANY)
+    widths = [STEP] * (n - 1) + [STEP + packed.shape[1] - width]
+    shapes = [
+        pltpu.VMEM((gate_slab.shape[1], 2 * hidden), bf),
+        pltpu.VMEM(down_slab.shape[1:], bf),
+        pltpu.VMEM((128 * rows, hidden), bf),
+        pltpu.VMEM((128 * rows, 2 * hidden), jnp.float32),
+        dma((3,)),
+        dma((n, 3, 2, 2)),
+        dma((n, 3, 2, 2)),
+        dma((n, 4, 2)),
+        dma((n, 3, 2, 2)),
+        dma((n, 3, 2, 2)),
+        dma((n, 2)),
+    ]
+    shapes += [pltpu.VMEM((2, 4, 4, 4, rows, w), bf) for w in widths]
+    shapes += [pltpu.VMEM((4, 4, 4, rows, STEP), bf)] * n
+    shapes += [pltpu.VMEM((2,) + (4,) * (2 - p) + (rows, STEP), bf) for _ in range(n) for p in range(3)]
+    shapes += [pltpu.VMEM((4,) * (2 - p) + (rows, STEP), bf) for _ in range(n) for p in range(3)]
     return pl.pallas_call(
-        lambda *refs: expert_kernel(side, depth, *refs),
+        expert_kernel,
         out_shape=jax.ShapeDtypeStruct((rows, width), jnp.float32),
         in_specs=[vmem, anywhere, anywhere, anywhere],
         out_specs=vmem,
-        scratch_shapes=[
-            pltpu.VMEM(gate_slab.shape[1:], jnp.bfloat16),
-            pltpu.VMEM(up_slab.shape[1:], jnp.bfloat16),
-            pltpu.VMEM(down_slab.shape[1:], jnp.bfloat16),
-            pltpu.VMEM((side, side, 2, depth * rows, packed.shape[1]), jnp.bfloat16),
-            pltpu.VMEM((count * rows, gate_slab.shape[2]), jnp.bfloat16),
-            pltpu.VMEM((count * rows, gate_slab.shape[2]), jnp.float32),
-            pltpu.VMEM((count * rows, gate_slab.shape[2]), jnp.float32),
-            dma((3,)),
-            dma((n, depth, 2)),
-            dma((n, side, side)),
-            dma((n, side, side, 2)),
-            dma((n, side, side, side, side)),
-            dma(()),
-        ]
-        + reduce_shapes(side, depth, rows, width),
+        scratch_shapes=shapes,
         compiler_params=pltpu.CompilerParams(
             collective_id=1, has_side_effects=True, vmem_limit_bytes=VMEM_LIMIT
         ),
@@ -553,13 +726,12 @@
 ):
     attended = attend(queries, new_keys, new_values, cache_keys, cache_values, cache_len)
     side = math.isqrt(lax.axis_size("ep") // 2)
-    depth = lax.axis_size("dp")
     labels = jnp.arange(router.shape[1], dtype=jnp.int32)
     chosen = jnp.any(expert_ids[:, :, None] == labels[None, None, :], axis=1).astype(jnp.float32)
     hidden, packed = project(
         side, attended, out_proj, resid, norm_gain.reshape(1, -1), router, chosen
     )
-    return hidden + run_experts(side, depth, packed, gate_slab, up_slab, down_slab)
+    return hidden + run_experts(packed, gate_slab, up_slab, down_slab)
 
 
 def solution(mesh):

time: 225 us -> 188 us (0.84)
  Pallas kernels: 211 us -> 174 us
    pallas_call x1, Pallas kernels: 172 us -> 135 us  [run_experts(): pl.pallas_call(expert_kernel, out_shape=jax.ShapeDtypeStruct((rows, width...]
where the time goes in v1:
time: 188 us
  Pallas kernels  174 us (93%)
  local copies, waits for them, and re-layouts  5.45 us (3%)
  matrix products  4.03 us (2%)
  other arithmetic  3.6 us (2%)
    pallas_call x1, Pallas kernels, run_experts(): pl.pallas_call(expert_kernel, out_shape=jax.ShapeDtypeStruct((rows, width...  135 us
    pallas_call x1, Pallas kernels, project(): pl.pallas_call(lambda *refs: projection_kernel(side, *refs), out_shape=(j...  39.4 us
    unnamed x10, local copies, waits for them, and re-layouts  3.99 us

profile of v1, /device:TPU:0, one launch (start us, length us, event | category | flops | bytes accessed | tf_op | source)
XLA Modules:
  0.0 187.7 jit_solution(14250809708198683374)
XLA Ops:
  0.0 0.7 iota_compare_fusion.1
  0.7 0.8 copy.21
  1.5 0.1 fusion.21
  1.6 0.6 convert_element_type.35.refs_5_
  2.2 0.7 reshape.55
  2.9 0.7 reshape.51
  3.7 1.0 copy.27
  4.7 0.0 copy-start.2
  4.7 0.2 fusion.25
  4.9 3.0 %fusion.24 = (f32[16,4,16]{2,1,0:T(4,128)S(1)}, f32[16,4,16,128]{3,2,1,0:T(8,128)S(1)}) fusion(bf16[16,4,16,128]{3,2,1,0:T(8,128)(2,1)S(1)} %bitcast.39, pred[16,128]{1,0:T(8,128)(4,1)S(1)} %iota_compare_fusion.1, bf16[16,128,512]{2,1,0:T(8,128)(2,1)} %param.18), kind=kOutput, calls=%fused_computation.24 | convolution fusion | flops 33946624 | bytes 2889728 | tf_op jit(solution)/shard_map/tgqd,tcgd->tgqc/dot_general | solution.py:26
  8.0 0.4 fusion.18
  8.5 0.0 copy-done.2
  8.5 0.0 copy-start
  8.5 0.8 fusion.15
  9.2 0.9 copy.48
  10.1 0.0 copy-done
  10.1 1.3 copy.22.refs_4_
  11.5 39.4 %shard_map.136 = (f32[16,4096]{1,0:T(8,128)}, bf16[16,4224]{1,0:T(8,128)(2,1)}) custom-call(bf16[16,8192]{1,0:T(8,128)(2,1)} %bitcast.40, bf16[256,4096]{1,0:T(8,128)(2,1)} %refs_1_.1, bf16[16,4096]{1,0:T(8,128)(2,1)} %refs_2_.1, f32[1,4096]{1,0:T(1,128)} %bitcast.45, bf16[4096,64]{1,0:T(8,128)(2,1)} %copy.22.refs_4_, f32[16,64]{1,0:T(8,128)} %convert_element_type.35.refs_5_), custom_call_target="tpu_custom_call" | custom-call | tf_op jit(solution)/shard_map/pallas_call | solution.py:321
  50.9 0.0 copy-start.1
  50.9 135.1 %shard_map.137 = f32[16,4096]{1,0:T(8,128)} custom-call(bf16[16,4224]{1,0:T(8,128)(2,1)} %get-tuple-element.8.own, bf16[1,4096,384]{2,1,0:T(8,128)(2,1)} %gate_hbm.1, bf16[1,4096,384]{2,1,0:T(8,128)(2,1)} %up_hbm.1, bf16[1,384,4096]{2,1,0:T(8,128)(2,1)} %down_hbm.1), custom_call_target="tpu_custom_call" | custom-call | tf_op jit(solution)/shard_map/pallas_call | solution.py:699
  186.0 0.0 copy-done.1
  186.0 1.7 add.11
  (2 shorter events, 0.1 us)
Async XLA Ops:
  4.7 3.8 %copy-start.2 = (bf16[16,128,512]{2,1,0:T(8,128)(2,1)S(1)}, bf16[16,128,512]{2,1,0:T(8,128)(2,1)}, u32[]{:S(2)}) copy-start(bf16[16,128,512]{2,1,0:T(8,128)(2,1)} %param.19) | copy-start | bytes 6291460
  8.5 1.6 copy-start
  50.9 135.1 %copy-start.1 = (f32[16,4096]{1,0:T(8,128)S(1)}, f32[16,4096]{1,0:T(8,128)}, u32[]{:S(2)}) copy-start(f32[16,4096]{1,0:T(8,128)} %get-tuple-element.7) | copy-start | bytes 786436

commit v2 on v1

--- a/solution.py
+++ b/solution.py
@@ -12,44 +12,6 @@
 KVH = 4
 HD = 128
 TOP = 8
-
-
-def attend(queries, new_keys, new_values, cache_keys, cache_values, cache_len):
-    local_rows = queries.shape[0]
-    cache_span = cache_keys.shape[1]
-    group_size = H // KVH
-    query_heads = queries.reshape(local_rows, KVH, group_size, HD)
-    past_keys = cache_keys.reshape(local_rows, cache_span, KVH, HD)
-    past_values = cache_values.reshape(local_rows, cache_span, KVH, HD)
-    score_scale = 1.0 / math.sqrt(HD)
-    past_scores = (
-        jnp.einsum("tgqd,tcgd->tgqc", query_heads, past_keys, preferred_element_type=jnp.float32)
-        * score_scale
-    )
-    own_scores = (
-        jnp.einsum(
-            "tgqd,tgd->tgq",
-            query_heads,
-            new_keys.reshape(local_rows, KVH, HD),
-            preferred_element_type=jnp.float32,
-        )
-        * score_scale
-    )
-    is_valid = lax.broadcasted_iota(jnp.int32, (local_rows, cache_span), 1) < cache_len[:, None]
-    past_scores = jnp.where(is_valid[:, None, None, :], past_scores, -1e30)
-    peak_score = jnp.maximum(jnp.max(past_scores, axis=3), own_scores)
-    past_exp = jnp.exp(past_scores - peak_score[..., None])
-    own_exp = jnp.exp(own_scores - peak_score)
-    denom_sum = jnp.sum(past_exp, axis=3) + own_exp
-    past_weights = (past_exp / denom_sum[..., None]).astype(jnp.bfloat16)
-    own_weights = (own_exp / denom_sum).astype(jnp.bfloat16)
-    blended = jnp.einsum(
-        "tgqc,tcgd->tgqd", past_weights, past_values, preferred_element_type=jnp.float32
-    )
-    blended = blended + own_weights.astype(jnp.float32)[..., None] * new_values.reshape(
-        local_rows, KVH, 1, HD
-    ).astype(jnp.float32)
-    return blended.reshape(local_rows, H * HD).astype(jnp.bfloat16)
 
 
 MESH = pl.DeviceIdType.MESH
@@ -246,28 +208,98 @@
     )
 
 
+def attend(queries, new_keys, new_values, keys, values, lengths, attended, qs, os, nk, nv):
+    tokens = queries.shape[0]
+    share = H // KVH
+    scale = 1.0 / math.sqrt(HD)
+    for h in range(H):
+        qs[tokens * h : tokens * h + tokens, :] = queries[:, HD * h : HD * h + HD].astype(jnp.float32)
+    nk[...] = new_keys[...].astype(jnp.float32)
+    nv[...] = new_values[...].astype(jnp.float32)
+
+    def spread(row):
+        return jnp.concatenate(
+            [jnp.broadcast_to(row[:, HD * g : HD * g + HD], (share, HD)) for g in range(KVH)], axis=0
+        )
+
+    def one(t):
+        rows = pl.ds(t, H, stride=tokens)
+        query = qs[rows, :]
+        narrow = query.astype(jnp.bfloat16)
+        scores = jnp.concatenate(
+            [
+                lax.dot_general(
+                    narrow[share * g : share * g + share],
+                    keys[t, :, HD * g : HD * g + HD],
+                    (((1,), (1,)), ((), ())),
+                    preferred_element_type=jnp.float32,
+                )
+                for g in range(KVH)
+            ],
+            axis=0,
+        )
+        own = jnp.sum(query * spread(nk[pl.ds(t, 1), :]), axis=1, keepdims=True) * scale
+        valid = lax.broadcasted_iota(jnp.int32, scores.shape, 1) < lengths[t]
+        scores = jnp.where(valid, scores * scale, -1e30)
+        peak = jnp.maximum(jnp.max(scores, axis=1, keepdims=True), own)
+        grown = jnp.exp(scores - peak)
+        own_grown = jnp.exp(own - peak)
+        denom = jnp.sum(grown, axis=1, keepdims=True) + own_grown
+        weights = (grown / denom).astype(jnp.bfloat16)
+        own_weight = (own_grown / denom).astype(jnp.bfloat16).astype(jnp.float32)
+        blended = jnp.concatenate(
+            [
+                jnp.dot(
+                    weights[share * g : share * g + share],
+                    values[t, :, HD * g : HD * g + HD],
+                    preferred_element_type=jnp.float32,
+                )
+                for g in range(KVH)
+            ],
+            axis=0,
+        )
+        os[rows, :] = blended + own_weight * spread(nv[pl.ds(t, 1), :])
+
+    def several(i, carry):
+        for k in range(4):
+            one(4 * i + k)
+        return carry
+
+    lax.fori_loop(0, tokens // 4, several, 0)
+    attended[...] = os[...].astype(jnp.bfloat16).reshape(attended.shape)
+
+
 def projection_kernel(
-    side, attended, weight_hbm, resid, gain, router, chosen, hidden, packed, weight, regrouped, part, wsem, ssem, rsem, *scratch
+    side, queries, new_keys, new_values, keys_hbm, values_hbm, lengths, weight_hbm, resid, gain, router, ids,
+    hidden, packed, attended, keys, values, qs, os, nk, nv, weight, regrouped, part, wsem, ssem, rsem, *scratch
 ):
     here = Place(side, 1)
-    rows = attended.shape[0]
+    rows = queries.shape[0]
     count = 2 * side * side
-    width = attended.shape[1] // count
     z = lax.axis_index("dp")
-    load = pltpu.make_async_copy(weight_hbm, weight, wsem)
+    caches = [
+        pltpu.make_async_copy(keys_hbm, keys, wsem.at[1]),
+        pltpu.make_async_copy(values_hbm, values, wsem.at[2]),
+    ]
+    load = pltpu.make_async_copy(weight_hbm, weight, wsem.at[0])
+    for copy in caches:
+        copy.start()
     load.start()
 
     def peer(j):
         return lax.rem(here.ep + j, count)
 
-    greet([(peer(j), z) for j in range(1, count)])
-
-    def piece(index):
-        return attended.at[:, pl.ds(pl.multiple_of(index * width, 128), width)]
+    barrier = pltpu.get_barrier_semaphore()
+    for j in range(1, count):
+        pl.semaphore_signal(barrier, inc=1, device_id=(peer(j), z), device_id_type=MESH)
+    for copy in caches:
+        copy.wait()
+    attend(queries, new_keys, new_values, keys, values, lengths, attended, qs, os, nk, nv)
+    pl.semaphore_wait(barrier, count - 1)
 
     def exchange(j, sending):
         return remote(
-            piece(peer(j)),
+            attended.at[peer(j)],
             regrouped.at[here.ep],
             ssem.at[j],
             rsem.at[count - j if sending else j],
@@ -276,15 +308,15 @@
 
     for j in range(1, count):
         exchange(j, True).start()
-    regrouped[here.ep] = attended[:, pl.ds(pl.multiple_of(here.ep * width, 128), width)]
+    regrouped[here.ep] = attended[here.ep]
     load.wait()
     for j in range(1, count):
         remote(
-            piece(peer(j)), regrouped.at[peer(j)], ssem.at[j], rsem.at[j], (peer(j), z)
+            attended.at[peer(j)], regrouped.at[peer(j)], ssem.at[j], rsem.at[j], (peer(j), z)
         ).wait_recv()
 
     def produce(s, cols):
-        left = regrouped[...].reshape(count * rows, width)
+        left = jnp.concatenate([regrouped[:, k].reshape(count * rows, HD) for k in range(2)], axis=1)
         return jnp.dot(left, weight[:, cols], preferred_element_type=jnp.float32)
 
     def finish(s, cols, total):
@@ -297,40 +329,55 @@
     reduce_scatter(here, rows, hidden.shape[1], produce, finish, (0, 2, 5, 8, 8), part, scratch)
     features = hidden.shape[1]
     scale = lax.rsqrt(jnp.maximum(sum(squares) / features, 0.25))
-    logits = jnp.zeros((rows, router.shape[1]), jnp.float32)
+    experts = router.shape[0]
+    logits = jnp.zeros((rows, experts), jnp.float32)
+    last_dims = (((1,), (1,)), ((), ()))
     for start, size in slices_of(features):
         cols = pl.ds(start, size)
         normed = (hidden[:, cols] * scale * gain[:, cols]).astype(jnp.bfloat16)
         packed[:, cols] = normed
-        logits = logits + jnp.dot(normed, router[cols, :], preferred_element_type=jnp.float32)
-    named = chosen[...] > 0
+        logits = logits + lax.dot_general(normed, router[:, cols], last_dims, preferred_element_type=jnp.float32)
+    label = lax.broadcasted_iota(jnp.int32, (experts, rows), 0)
+    marks = sum((ids[k : k + 1, :] == label).astype(jnp.float32) for k in range(TOP))
+    eye = (
+        lax.broadcasted_iota(jnp.int32, (rows, rows), 0) == lax.broadcasted_iota(jnp.int32, (rows, rows), 1)
+    ).astype(jnp.float32)
+    named = lax.dot_general(eye, marks, last_dims, preferred_element_type=jnp.float32) > 0.5
     peak = jnp.max(jnp.where(named, logits, -jnp.inf), axis=1, keepdims=True)
     grown = jnp.where(named, jnp.exp(jnp.where(named, logits - peak, 0.0)), 0.0)
     probs = grown / jnp.sum(grown, axis=1, keepdims=True)
     packed[:, features:] = jnp.zeros((rows, packed.shape[1] - features), jnp.bfloat16)
-    packed[:, features : features + router.shape[1]] = probs.astype(jnp.bfloat16)
+    packed[:, features : features + experts] = probs.astype(jnp.bfloat16)
     for j in range(1, count):
         exchange(j, True).wait_send()
 
 
-def project(side, attended, out_proj, resid, gain, router, chosen):
+def project(side, queries, new_keys, new_values, cache_keys, cache_values, cache_len, out_proj, resid, gain, router, ids):
     rows, width = resid.shape
     count = 2 * side * side
-    dma = pltpu.SemaphoreType.DMA
-    vmem = pl.BlockSpec(memory_space=pltpu.VMEM)
+    dma, bf = pltpu.SemaphoreType.DMA, jnp.bfloat16
+    vmem, anywhere = pl.BlockSpec(memory_space=pltpu.VMEM), pl.BlockSpec(memory_space=pl.ANY)
     return pl.pallas_call(
         lambda *refs: projection_kernel(side, *refs),
         out_shape=(
             jax.ShapeDtypeStruct((rows, width), jnp.float32),
-            jax.ShapeDtypeStruct((rows, width + pl.cdiv(router.shape[1], 128) * 128), jnp.bfloat16),
+            jax.ShapeDtypeStruct((rows, width + pl.cdiv(router.shape[0], 128) * 128), bf),
         ),
-        in_specs=[vmem, pl.BlockSpec(memory_space=pl.ANY), vmem, vmem, vmem, vmem],
+        in_specs=[vmem, vmem, vmem, anywhere, anywhere, pl.BlockSpec(memory_space=pltpu.SMEM), anywhere]
+        + [vmem] * 4,
         out_specs=(vmem, vmem),
         scratch_shapes=[
-            pltpu.VMEM(out_proj.shape, jnp.bfloat16),
-            pltpu.VMEM((count, rows, attended.shape[1] // count), jnp.bfloat16),
-            pltpu.VMEM((side, side, 2, rows, width), jnp.bfloat16),
-            dma(()),
+            pltpu.VMEM((count, H // count, rows, HD), bf),
+            pltpu.VMEM(cache_keys.shape, bf),
+            pltpu.VMEM(cache_values.shape, bf),
+            pltpu.VMEM((H * rows, HD), jnp.float32),
+            pltpu.VMEM((H * rows, HD), jnp.float32),
+            pltpu.VMEM(new_keys.shape, jnp.float32),
+            pltpu.VMEM(new_values.shape, jnp.float32),
+            pltpu.VMEM(out_proj.shape, bf),
+            pltpu.VMEM((count, H // count, rows, HD), bf),
+            pltpu.VMEM((side, side, 2, rows, width), bf),
+            dma((3,)),
             dma((count,)),
             dma((count,)),
         ]
@@ -338,22 +385,14 @@
         compiler_params=pltpu.CompilerParams(
             collective_id=0, has_side_effects=True, vmem_limit_bytes=VMEM_LIMIT
         ),
-    )(attended, out_proj, resid, gain, router, chosen)
+    )(queries, new_keys, new_values, cache_keys, cache_values, cache_len, out_proj, resid, gain, router, ids)
 
 
 AXES = ("y", "x", "z")
-ORDERS = (
-    ("y", "x", "z"),
-    ("z", "x", "y"),
-    ("y", "z", "x"),
-    ("y", "x", "z"),
-    ("z", "x", "y"),
-    ("y", "z", "x"),
-    ("y", "x", "z"),
-    ("z", "x", "y"),
-)
-STEP = 512
-HALF = 256
+TURNS = (("x", "y", "z"), ("y", "z", "x"), ("z", "x", "y"))
+ORDERS = TURNS * 3
+WIDTHS = (512,) * 6 + (384, 384, 256)
+STARTS = tuple(sum(WIDTHS[:s]) for s in range(len(WIDTHS)))
 
 
 class Spot:
@@ -401,10 +440,11 @@
         sends.append(copy)
 
     def cols_of(s):
-        return pl.ds(STEP * s, held[s].shape[-1])
-
-    def halves(s, d, width):
-        return (slice(None),) * 1 + (pl.ds(0, HALF) if d == 0 else pl.ds(HALF, width - HALF),)
+        return pl.ds(STARTS[s], held[s].shape[-1])
+
+    def halves(width, d):
+        cut = 256 if width > 256 else 128
+        return (slice(None), pl.ds(0, cut) if d == 0 else pl.ds(cut, width - cut))
 
     def spread_index(s, p, off, core=None):
         order = ORDERS[s]
@@ -417,35 +457,44 @@
 
     def spread_half(s, p, off, d):
         width = held[s].shape[-1]
-        return held[s].at[spread_index(s, p, off) + halves(s, d, width)]
+        return held[s].at[spread_index(s, p, off) + halves(width, d)]
 
     def direct_gather(s, p):
-        return p == 0 or (p == 1 and s < 3)
+        return p == 0 or (p == 1 and s < 3) or (p == 2 and s >= 6)
+
+    def near_gather(s, p, d, h, sending):
+        axis = ORDERS[s][p]
+        off = (1, 3)[d]
+        ref = spread_half(s, p, 0 if sending else 4 - off, h)
+        return remote(
+            ref, ref, nsem.at[s, p, d, h, 0], nsem.at[s, p, d, h, 1], here.at(axis, off if sending else 4 - off)
+        )
 
     def gather_near(s, p):
         axis = ORDERS[s][p]
-        for d, off in enumerate((1, 3)):
-            src = own.at[:, cols_of(s)] if p == 0 else spread(s, p, 0)
-            go(remote(src, spread(s, p, 0), nsem.at[s, p, d, 0], nsem.at[s, p, d, 1], here.at(axis, off)))
+        for h in range(2):
+            for d in range(2):
+                go(near_gather(s, p, d, (d + h) % 2, True))
         if direct_gather(s, p):
-            src = own.at[:, cols_of(s)] if p == 0 else spread(s, p, 0)
-            go(remote(src, spread(s, p, 0), fsem.at[s, p, 0, 0], fsem.at[s, p, 0, 1], here.at(axis, 2)))
+            ref = spread(s, p, 0)
+            go(remote(ref, ref, fsem.at[s, p, 0, 0], fsem.at[s, p, 0, 1], here.at(axis, 2)))
         if p == 2:
             give(s, 0, 0)
 
     def gather_far(s, p):
         axis = ORDERS[s][p]
         for d, (off, back) in enumerate(((1, 3), (3, 1))):
-            ref = spread(s, p, back)
-            remote(ref, ref, nsem.at[s, p, d, 0], nsem.at[s, p, d, 1], here.at(axis, back)).wait_recv()
+            near_gather(s, p, d, d, False).wait_recv()
             if not direct_gather(s, p):
                 ref = spread_half(s, p, back, d)
                 go(remote(ref, ref, fsem.at[s, p, d, 0], fsem.at[s, p, d, 1], here.at(axis, off)))
+
+    def gather_end(s, p):
+        axis = ORDERS[s][p]
+        for d, back in enumerate((3, 1)):
+            near_gather(s, p, d, 1 - d, False).wait_recv()
             if p == 2:
                 give(s, 1 + d, back)
-
-    def gather_end(s, p):
-        axis = ORDERS[s][p]
         if direct_gather(s, p):
             ref = spread(s, p, 2)
             remote(ref, ref, fsem.at[s, p, 0, 0], fsem.at[s, p, 0, 1], here.at(axis, 2)).wait_recv()
@@ -470,14 +519,17 @@
     def rows_at(i):
         return pl.ds(pl.multiple_of(i * group, group), group)
 
+    def span(s):
+        return slice(STARTS[s], STARTS[s] + WIDTHS[s])
+
     def consume(s):
         if s == 0:
             loads[0].wait()
             loads[1].wait()
 
         def step(i, carry):
-            block = held[s][i // 2, pl.ds(2 * lax.rem(i, 2), 2), :, :, :, :STEP].reshape(group, STEP)
-            value = jnp.dot(block, gu[STEP * s : STEP * s + STEP, :], preferred_element_type=jnp.float32)
+            block = held[s][i // 2, pl.ds(2 * lax.rem(i, 2), 2), :, :, :, : WIDTHS[s]].reshape(group, WIDTHS[s])
+            value = jnp.dot(block, gu[span(s), :], preferred_element_type=jnp.float32)
             total[rows_at(i), :] = value if s == 0 else total[rows_at(i), :] + value
             return carry
 
@@ -492,31 +544,39 @@
         gather_end(s, 0)
         gather_near(s, 1)
 
+    def second_far(s):
+        gather_far(s, 1)
+
     def third(s):
-        gather_far(s, 1)
-
-    def fourth(s):
         gather_end(s, 1)
         gather_near(s, 2)
 
-    def fifth(s):
+    def third_far(s):
         gather_far(s, 2)
 
-    def sixth(s):
+    def last(s):
         gather_end(s, 2)
+
+    def use(s):
         take(s)
         consume(s)
 
-    groups = ((0, 1, 2), (3, 4, 5), (6, 7))
-    plan = (
-        (start, 0), (start, 1), (start, 2),
-        (second, 0), (second, 1), (third, 0), (second, 2), (fourth, 0),
-        (third, 1), (fourth, 1), (third, 2), (fifth, 0), (fourth, 2),
-        (sixth, 0), (fifth, 1), (sixth, 1), (fifth, 2), (sixth, 2),
+    def run(*steps):
+        for phase, group_of in steps:
+            for s in group_of:
+                phase(s)
+
+    run(
+        (start, range(n)), (second, (0, 1, 2)), (second, (3, 4, 5)), (second_far, (0, 1, 2)), (third, (0, 1, 2)),
+        (second_far, (3, 4, 5)), (second, (6, 7, 8)), (third_far, (0, 1, 2)), (third, (3, 4, 5)),
+        (second_far, (6, 7, 8)), (last, (0, 1, 2)),
     )
-    for phase, g in plan:
-        for s in groups[g]:
-            phase(s)
+    for s in range(3):
+        run((use, (s,)), (third_far, (3 + s,)), (third, (6 + s,)))
+    run((last, (3, 4, 5)))
+    for s in range(3, 6):
+        run((use, (s,)), (third_far, (3 + s,)))
+    run((last, (6, 7, 8)), (use, (6, 7, 8)))
     for copy in sends:
         copy.wait_send()
     sends.clear()
@@ -524,7 +584,7 @@
     expert = (lax.axis_index("ep") * 4 + here.pos["z"]) // 2
 
     def activate(i, carry):
-        tail = held[n - 1][i // 2, pl.ds(2 * lax.rem(i, 2), 2), :, :, :, STEP:].reshape(group, 128)
+        tail = held[n - 1][i // 2, pl.ds(2 * lax.rem(i, 2), 2), :, :, :, WIDTHS[n - 1] :].reshape(group, 128)
         lane = lax.broadcasted_iota(jnp.int32, tail.shape, 1)
         weight = jnp.sum(jnp.where(lane == expert, tail.astype(jnp.float32), 0.0), axis=1, keepdims=True)
         gate_val = total[rows_at(i), :hidden]
@@ -541,18 +601,18 @@
         return here.index(fixed)
 
     def direct_fold(s, p):
-        return p == 2 or (p == 1 and s >= n - 2)
+        return p >= 1
 
     def gain(s, p, off):
         index = fold(s, p, off)
         if p == 0:
-            mine = held[s][(here.core,) + index + (slice(None), pl.ds(0, STEP))]
+            mine = held[s][(here.core,) + index + (slice(None), pl.ds(0, WIDTHS[s]))]
             return mine + inner[s][index]
         return inner[s][index]
 
     def core_copy(s):
         return remote(
-            held[s].at[1 - here.core, :, :, :, :, pl.ds(0, STEP)],
+            held[s].at[1 - here.core, :, :, :, :, pl.ds(0, WIDTHS[s])],
             inner[s],
             rcore.at[s, 0],
             rcore.at[s, 1],
@@ -564,10 +624,10 @@
             def one(h, carry):
                 i = 2 * core + h
                 value = jnp.dot(
-                    act[rows_at(i), :], down[:, STEP * s : STEP * s + STEP], preferred_element_type=jnp.float32
+                    act[rows_at(i), :], down[:, span(s)], preferred_element_type=jnp.float32
                 )
-                held[s][core, pl.ds(2 * h, 2), :, :, :, :STEP] = value.astype(jnp.bfloat16).reshape(
-                    2, 4, 4, rows, STEP
+                held[s][core, pl.ds(2 * h, 2), :, :, :, : WIDTHS[s]] = value.astype(jnp.bfloat16).reshape(
+                    2, 4, 4, rows, WIDTHS[s]
                 )
                 return carry
 
@@ -577,8 +637,8 @@
         go(core_copy(s))
         step(here.core)
 
-    def half_of(ref, index, d):
-        return ref.at[index + (slice(None), pl.ds(HALF * d, HALF))]
+    def half_of(s, ref, index, d):
+        return ref.at[index + halves(WIDTHS[s], d)]
 
     def lead(p):
         return (slice(None),) * (2 - p)
@@ -591,21 +651,21 @@
                 inner[s].at[index], fars[s][p], rfar.at[s, p, 0, 0], rfar.at[s, p, 0, 1], here.at(axis, 2)
             )
         return remote(
-            half_of(inner[s], index, d),
-            half_of(fars[s][p], lead(p), d),
+            half_of(s, inner[s], index, d),
+            half_of(s, fars[s][p], lead(p), d),
             rfar.at[s, p, d, 0],
             rfar.at[s, p, d, 1],
             here.at(axis, (1, 3)[d]),
         )
 
-    def near_copy(s, p, d):
+    def near_copy(s, p, d, h):
         axis = ORDERS[s][2 - p]
         off = (1, 3)[d]
         return remote(
-            inner[s].at[fold(s, p, off)],
-            nears[s][p].at[d],
-            rnear.at[s, p, d, 0],
-            rnear.at[s, p, d, 1],
+            half_of(s, inner[s], fold(s, p, off), h),
+            half_of(s, nears[s][p], (d,) + lead(p), h),
+            rnear.at[s, p, d, h, 0],
+            rnear.at[s, p, d, h, 1],
             here.at(axis, off),
         )
 
@@ -613,56 +673,47 @@
         if p == 0:
             core_copy(s).wait_recv()
             inner[s][fold(s, 0, 2)] = gain(s, 0, 2)
-        if direct_fold(s, p):
-            go(far_copy(s, p, 0, True))
-            fold_near(s, p)
-        else:
-            for d in range(2):
-                go(far_copy(s, p, d, True))
+        for d in range(1 if direct_fold(s, p) else 2):
+            go(far_copy(s, p, d, True))
+        for d, off in enumerate((1, 3)):
+            if p == 0:
+                inner[s][fold(s, p, off)] = gain(s, p, off)
+            go(near_copy(s, p, d, 1 - d))
+            if direct_fold(s, p):
+                go(near_copy(s, p, d, d))
 
     def fold_near(s, p):
         for d, off in enumerate((1, 3)):
-            index = fold(s, p, off)
-            if direct_fold(s, p):
-                if p == 0:
-                    inner[s][index] = gain(s, p, off)
-            else:
-                far_copy(s, p, d, False).wait_recv()
-                if p == 0:
-                    inner[s][index] = gain(s, p, off)
-                part = index + (slice(None), pl.ds(HALF * d, HALF))
-                inner[s][part] = inner[s][part] + fars[s][p][lead(p) + (slice(None), pl.ds(HALF * d, HALF))]
-            go(near_copy(s, p, d))
+            far_copy(s, p, d, False).wait_recv()
+            part = fold(s, p, off) + halves(WIDTHS[s], d)
+            inner[s][part] = inner[s][part] + fars[s][p][lead(p) + halves(WIDTHS[s], d)]
+            go(near_copy(s, p, d, d))
 
     def fold_end(s, p):
         value = gain(s, p, 0).astype(jnp.float32)
         for d in range(2):
-            near_copy(s, p, d).wait_recv()
+            for h in range(2):
+                near_copy(s, p, d, h).wait_recv()
             value = value + nears[s][p][d].astype(jnp.float32)
         if direct_fold(s, p):
             far_copy(s, p, 0, False).wait_recv()
             value = value + fars[s][p][...].astype(jnp.float32)
         if p == 2:
-            mixed[:, STEP * s : STEP * s + STEP] = value
+            mixed[:, span(s)] = value
         else:
             inner[s][fold(s, p, 0)] = value.astype(jnp.bfloat16)
 
     def next_fold(s, p):
         fold_end(s, p - 1)
         fold_far(s, p)
-
-    def middle(s):
-        if not direct_fold(s, 1):
-            fold_near(s, 1)
 
     phases = (
         (produce, 0),
         (lambda s: fold_far(s, 0), 1),
         (lambda s: fold_near(s, 0), 3),
         (lambda s: next_fold(s, 1), 5),
-        (middle, 6),
         (lambda s: next_fold(s, 2), 7),
-        (lambda s: fold_end(s, 2), 8),
+        (lambda s: fold_end(s, 2), 9),
     )
     for step in range(n + phases[-1][1]):
         for phase, lag in phases:
@@ -678,24 +729,24 @@
     n = len(ORDERS)
     dma, bf = pltpu.SemaphoreType.DMA, jnp.bfloat16
     vmem, anywhere = pl.BlockSpec(memory_space=pltpu.VMEM), pl.BlockSpec(memory_space=pl.ANY)
-    widths = [STEP] * (n - 1) + [STEP + packed.shape[1] - width]
+    extra = packed.shape[1] - width
     shapes = [
         pltpu.VMEM((gate_slab.shape[1], 2 * hidden), bf),
         pltpu.VMEM(down_slab.shape[1:], bf),
         pltpu.VMEM((128 * rows, hidden), bf),
         pltpu.VMEM((128 * rows, 2 * hidden), jnp.float32),
         dma((3,)),
-        dma((n, 3, 2, 2)),
+        dma((n, 3, 2, 2, 2)),
         dma((n, 3, 2, 2)),
         dma((n, 4, 2)),
-        dma((n, 3, 2, 2)),
+        dma((n, 3, 2, 2, 2)),
         dma((n, 3, 2, 2)),
         dma((n, 2)),
     ]
-    shapes += [pltpu.VMEM((2, 4, 4, 4, rows, w), bf) for w in widths]
-    shapes += [pltpu.VMEM((4, 4, 4, rows, STEP), bf)] * n
-    shapes += [pltpu.VMEM((2,) + (4,) * (2 - p) + (rows, STEP), bf) for _ in range(n) for p in range(3)]
-    shapes += [pltpu.VMEM((4,) * (2 - p) + (rows, STEP), bf) for _ in range(n) for p in range(3)]
+    shapes += [pltpu.VMEM((2, 4, 4, 4, rows, w + extra * (s == n - 1)), bf) for s, w in enumerate(WIDTHS)]
+    shapes += [pltpu.VMEM((4, 4, 4, rows, w), bf) for w in WIDTHS]
+    shapes += [pltpu.VMEM((2,) + (4,) * (2 - p) + (rows, w), bf) for w in WIDTHS for p in range(3)]
+    shapes += [pltpu.VMEM((4,) * (2 - p) + (rows, w), bf) for w in WIDTHS for p in range(3)]
     return pl.pallas_call(
         expert_kernel,
         out_shape=jax.ShapeDtypeStruct((rows, width), jnp.float32),
@@ -724,12 +775,10 @@
     up_slab,
     down_slab,
 ):
-    attended = attend(queries, new_keys, new_values, cache_keys, cache_values, cache_len)
     side = math.isqrt(lax.axis_size("ep") // 2)
-    labels = jnp.arange(router.shape[1], dtype=jnp.int32)
-    chosen = jnp.any(expert_ids[:, :, None] == labels[None, None, :], axis=1).astype(jnp.float32)
     hidden, packed = project(
-        side, attended, out_proj, resid, norm_gain.reshape(1, -1), router, chosen
+        side, queries, new_keys, new_values, cache_keys, cache_values, cache_len,
+        out_proj, resid, norm_gain.reshape(1, -1), router.T, expert_ids.T,
     )
     return hidden + run_experts(packed, gate_slab, up_slab, down_slab)
 

time: 188 us -> 158 us (0.84)
  Pallas kernels: 174 us -> 156 us
  local copies, waits for them, and re-layouts: 5.45 us -> 0.01 us
  matrix products: 4.03 us -> 0 us
  other arithmetic: 3.6 us -> 1.69 us
    pallas_call x1, Pallas kernels: 135 us -> 112 us  [run_experts(): pl.pallas_call(expert_kernel, out_shape=jax.ShapeDtypeStruct((rows, width...]
    pallas_call x1, Pallas kernels: 39.4 us -> 44.8 us  [project(): pl.pallas_call(lambda *refs: projection_kernel(side, *refs), out_shape=(j...]
    dot_general x3 -> x0, matrix products: 4.03 us -> none  [the longest x1 3.03 us: attend(): jnp.einsum('tgqd,tcgd->tgqc', query_heads, past_keys, preferred_element_t...]
    unnamed x10 -> x2, local copies, waits for them, and re-layouts: 3.99 us -> 0.01 us
where the time goes in v2:
time: 158 us
  Pallas kernels  156 us (99%)
  other arithmetic  1.69 us (1%)
    pallas_call x1, Pallas kernels, run_experts(): pl.pallas_call(expert_kernel, out_shape=jax.ShapeDtypeStruct((rows, width...  112 us
    pallas_call x1, Pallas kernels, project(): pl.pallas_call(lambda *refs: projection_kernel(side, *refs), out_shape=(j...  44.8 us

profile of v2, /device:TPU:0, one launch (start us, length us, event | category | flops | bytes accessed | tf_op | source)
XLA Modules:
  0.0 158.1 jit_solution(12282942784356223449)
XLA Ops:
  0.0 44.8 %shard_map.136 = (f32[16,4096]{1,0:T(8,128)}, bf16[16,4224]{1,0:T(8,128)(2,1)}) custom-call(bf16[16,8192]{1,0:T(8,128)(2,1)} %refs_0_.1, bf16[16,512]{1,0:T(8,128)(2,1)} %refs_1_.1, bf16[16,512]{1,0:T(8,128)(2,1)} %refs_2_.1, bf16[16,128,512]{2,1,0:T(8,128)(2,1)} %refs_3_.1, bf16[16,128,512]{2,1,0:T(8,128)(2,1)} %refs_4_.1, s32[16]{0:T(128)} %refs_5_.1, ...), custom_call_target="tpu_custom_call" | custom-call | tf_op jit(solution)/shard_map/pallas_call | solution.py:360
  44.8 0.0 copy-start
  44.8 111.6 %shard_map.137 = f32[16,4096]{1,0:T(8,128)} custom-call(bf16[16,4224]{1,0:T(8,128)(2,1)} %get-tuple-element.8.own, bf16[1,4096,384]{2,1,0:T(8,128)(2,1)} %gate_hbm.1, bf16[1,4096,384]{2,1,0:T(8,128)(2,1)} %up_hbm.1, bf16[1,384,4096]{2,1,0:T(8,128)(2,1)} %down_hbm.1), custom_call_target="tpu_custom_call" | custom-call | tf_op jit(solution)/shard_map/pallas_call | solution.py:750
  156.4 0.0 copy-done
  156.4 1.7 %add.3 = f32[16,4096]{1,0:T(8,128)} add(f32[16,4096]{1,0:T(8,128)S(1)} %copy-done, f32[16,4096]{1,0:T(8,128)} %shard_map.137) | non-fusion elementwise | flops 65536 | bytes 786432 | tf_op jit(solution)/shard_map/add | solution.py:783
Async XLA Ops:
  44.8 111.6 %copy-start = (f32[16,4096]{1,0:T(8,128)S(1)}, f32[16,4096]{1,0:T(8,128)}, u32[]{:S(2)}) copy-start(f32[16,4096]{1,0:T(8,128)} %get-tuple-element.7) | copy-start | bytes 786436

commit v3 on v2

v3 whole, which is shorter than its diff:
```python
import math

import jax
import jax.numpy as jnp
from jax import lax
from jax.experimental import pallas as pl
from jax.experimental.pallas import tpu as pltpu
from jax.sharding import PartitionSpec as P

D = 4096
H = 64
KVH = 4
HD = 128
TOP = 8
CAP = 4


MESH = pl.DeviceIdType.MESH
VMEM_LIMIT = 66_000_000


def remote(src, dst, send, recv, device):
    return pltpu.make_async_remote_copy(
        src_ref=src, dst_ref=dst, send_sem=send, recv_sem=recv, device_id=device, device_id_type=MESH
    )


def attend(queries, new_keys, new_values, keys, values, lengths, attended, qs, os, nk, nv):
    tokens = queries.shape[0]
    share = H // KVH
    scale = 1.0 / math.sqrt(HD)
    for h in range(H):
        qs[tokens * h : tokens * h + tokens, :] = queries[:, HD * h : HD * h + HD].astype(jnp.float32)
    nk[...] = new_keys[...].astype(jnp.float32)
    nv[...] = new_values[...].astype(jnp.float32)

    def spread(row):
        return jnp.concatenate(
            [jnp.broadcast_to(row[:, HD * g : HD * g + HD], (share, HD)) for g in range(KVH)], axis=0
        )

    def one(t):
        rows = pl.ds(t, H, stride=tokens)
        query = qs[rows, :]
        narrow = query.astype(jnp.bfloat16)
        scores = jnp.concatenate(
            [
                lax.dot_general(
                    narrow[share * g : share * g + share],
                    keys[t, :, HD * g : HD * g + HD],
                    (((1,), (1,)), ((), ())),
                    preferred_element_type=jnp.float32,
                )
                for g in range(KVH)
            ],
            axis=0,
        )
        own = jnp.sum(query * spread(nk[pl.ds(t, 1), :]), axis=1, keepdims=True) * scale
        valid = lax.broadcasted_iota(jnp.int32, scores.shape, 1) < lengths[t]
        scores = jnp.where(valid, scores * scale, -1e30)
        peak = jnp.maximum(jnp.max(scores, axis=1, keepdims=True), own)
        grown = jnp.exp(scores - peak)
        own_grown = jnp.exp(own - peak)
        denom = jnp.sum(grown, axis=1, keepdims=True) + own_grown
        weights = (grown / denom).astype(jnp.bfloat16)
        own_weight = (own_grown / denom).astype(jnp.bfloat16).astype(jnp.float32)
        blended = jnp.concatenate(
            [
                jnp.dot(
                    weights[share * g : share * g + share],
                    values[t, :, HD * g : HD * g + HD],
                    preferred_element_type=jnp.float32,
                )
                for g in range(KVH)
            ],
            axis=0,
        )
        os[rows, :] = blended + own_weight * spread(nv[pl.ds(t, 1), :])

    def several(i, carry):
        for k in range(4):
            one(4 * i + k)
        return carry

    lax.fori_loop(0, tokens // 4, several, 0)
    attended[...] = os[...].astype(jnp.bfloat16).reshape(attended.shape)


AXES = ("y", "x", "z")
TURNS = (("x", "y", "z"), ("y", "z", "x"), ("z", "x", "y"))
ORDERS = TURNS * 3
WIDTHS = (512,) * 6 + (384, 384, 256)
STARTS = tuple(sum(WIDTHS[:s]) for s in range(len(WIDTHS)))


class Spot:
    def __init__(self):
        ep = lax.axis_index("ep")
        self.core = lax.rem(ep, 2)
        self.pos = {"x": lax.rem(ep // 2, 4), "y": ep // 8, "z": lax.axis_index("dp")}

    def coord(self, axis, off):
        return lax.rem(self.pos[axis] + off, 4) if off else self.pos[axis]

    def at(self, axis=None, off=0, flip=False):
        place = dict(self.pos)
        if axis:
            place[axis] = self.coord(axis, off)
        core = 1 - self.core if flip else self.core
        return ((place["y"] * 4 + place["x"]) * 2 + core, place["z"])

    def plane(self, dy, dx):
        return ((self.coord("y", dy) * 4 + self.coord("x", dx)) * 2 + self.core, self.pos["z"])

    def index(self, fixed):
        return tuple(fixed.get(axis, slice(None)) for axis in AXES)


LAGS = (0, 2, 5, 8)


def layer_kernel(
    queries, new_keys, new_values, keys_hbm, values_hbm, lengths, weight_hbm, resid, gain, router, ids,
    gate_hbm, up_hbm, down_hbm, mixed,
    own, attended, keys, values, qs, os, nk, nv, weight, regrouped, in2, sum2, in3, asem, osem, psem, qsem, tsem,
    gu, down, act, total, picked, sel, back, wsem, nsem, fsem, csem, rnear, rfar, rcore, *scratch
):
    n = len(ORDERS)
    held, inner = scratch[:n], scratch[n : 2 * n]
    nears = [scratch[2 * n + 3 * s : 2 * n + 3 * s + 3] for s in range(n)]
    fars = [scratch[5 * n + 3 * s : 5 * n + 3 * s + 3] for s in range(n)]
    here = Spot()
    rows = own.shape[0]
    hidden = act.shape[1]
    experts = router.shape[0]
    count = 32
    ep, z = lax.axis_index("ep"), lax.axis_index("dp")
    caches = [
        pltpu.make_async_copy(keys_hbm, keys, asem.at[0]),
        pltpu.make_async_copy(values_hbm, values, asem.at[1]),
        pltpu.make_async_copy(weight_hbm, weight, asem.at[2]),
    ]
    loads = [
        pltpu.make_async_copy(gate_hbm.at[0], gu.at[:, pl.ds(0, hidden)], wsem.at[0]),
        pltpu.make_async_copy(up_hbm.at[0], gu.at[:, pl.ds(hidden, hidden)], wsem.at[1]),
        pltpu.make_async_copy(down_hbm.at[0], down, wsem.at[2]),
    ]
    for load in caches + loads:
        load.start()

    def peer(j):
        return lax.rem(ep + j, count)

    barrier = pltpu.get_barrier_semaphore()
    everyone = [(peer(j), z) for j in range(1, count)] + [here.at("z", off) for off in (1, 2, 3)]
    for device in everyone:
        pl.semaphore_signal(barrier, inc=1, device_id=device, device_id_type=MESH)
    caches[0].wait()
    caches[1].wait()
    attend(queries, new_keys, new_values, keys, values, lengths, attended, qs, os, nk, nv)
    pl.semaphore_wait(barrier, len(everyone))
    sends, early = [], []

    def go(copy, kept=sends):
        copy.start()
        kept.append(copy)

    for j in range(1, count):
        go(remote(attended.at[peer(j)], regrouped.at[ep], osem.at[j, 0], osem.at[count - j, 1], (peer(j), z)), early)
    regrouped[ep] = attended[ep]
    caches[2].wait()
    for j in range(1, count):
        remote(attended.at[peer(j)], regrouped.at[peer(j)], osem.at[j, 0], osem.at[j, 1], (peer(j), z)).wait_recv()

    def pair_copy(s):
        return remote(
            inner[s].at[:, :, 1 - here.core], inner[s].at[:, :, 2], psem.at[s, 0], psem.at[s, 1], here.at(flip=True)
        )

    def turn(s, a, b):
        return (a, b) if s % 2 == 0 else (b, a)

    def line(s, a, b):
        dy, dx = turn(s, a, b)
        return here.coord("y", dy), here.coord("x", dx)

    def columns(s):
        return pl.ds(STARTS[s], WIDTHS[s])

    def first_copy(s, ja, kb, sending):
        y, x = line(s, ja, kb)
        return remote(
            inner[s].at[y, x, 2],
            in2.at[3 - ja, kb, :, columns(s)],
            qsem.at[s, ja, kb, 0],
            qsem.at[s, 4 - ja if sending else ja, kb, 1],
            here.plane(*turn(s, ja, 0)),
        )

    def second_copy(s, kb, sending):
        return remote(
            sum2.at[kb, :, columns(s)],
            in3.at[3 - kb, :, columns(s)],
            tsem.at[s, kb, 0],
            tsem.at[s, 4 - kb if sending else kb, 1],
            here.plane(*turn(s, 0, kb)),
        )

    def wide(value):
        return value.astype(jnp.float32)

    def phase0(s):
        left = jnp.concatenate([regrouped[:, k].reshape(count * rows, HD) for k in range(2)], axis=1)
        value = jnp.dot(left, weight[:, columns(s)], preferred_element_type=jnp.float32)
        inner[s][:, :, 0:2] = value.astype(jnp.bfloat16).reshape(4, 4, 2, rows, WIDTHS[s])
        go(pair_copy(s), early)

    def phase1(s):
        pair_copy(s).wait_recv()
        for a in (1, 2, 3, 0):
            for b in (1, 2, 3, 0):
                y, x = line(s, a, b)
                inner[s][y, x, 2] = (wide(inner[s][y, x, here.core]) + wide(inner[s][y, x, 2])).astype(jnp.bfloat16)
                if a:
                    go(first_copy(s, a, b, True), early)

    def phase2(s):
        for b in (1, 2, 3, 0):
            y, x = line(s, 0, b)
            value = wide(inner[s][y, x, 2])
            for a in range(1, 4):
                first_copy(s, a, b, False).wait_recv()
                value = value + wide(in2[a - 1, b, :, columns(s)])
            sum2[b, :, columns(s)] = value.astype(jnp.bfloat16)
            if b:
                go(second_copy(s, b, True), early)

    def phase3(s):
        value = wide(sum2[0, :, columns(s)])
        for b in range(1, 4):
            second_copy(s, b, False).wait_recv()
            value = value + wide(in3[b - 1, :, columns(s)])
        value = wide(resid[:, columns(s)]) + value
        mixed[:, columns(s)] = value
        squares.append(jnp.sum(value * value, axis=1, keepdims=True))
        scaled = (value * gain[:, columns(s)]).astype(jnp.bfloat16)
        own[:, columns(s)] = scaled
        logits.append(
            lax.dot_general(scaled, router[:, columns(s)], (((1,), (1,)), ((), ())), preferred_element_type=jnp.float32)
        )
        if s < n - 1:
            start(s)
        if s >= 3:
            second(s - 3)
        if s >= 6:
            second_far(s - 6)
            third(s - 6)

    def find():
        label = lax.broadcasted_iota(jnp.int32, (experts, rows), 0)
        marks = sum((ids[k : k + 1, :] == label).astype(jnp.float32) for k in range(TOP))
        eye = (
            lax.broadcasted_iota(jnp.int32, (rows, rows), 0) == lax.broadcasted_iota(jnp.int32, (rows, rows), 1)
        ).astype(jnp.float32)
        return lax.dot_general(eye, marks, (((1,), (1,)), ((), ())), preferred_element_type=jnp.float32) > 0.5

    def route(named, logit):
        peak = jnp.max(jnp.where(named, logit, -jnp.inf), axis=1, keepdims=True)
        grown = jnp.where(named, jnp.exp(jnp.where(named, logit - peak, 0.0)), 0.0)
        return grown / jnp.sum(grown, axis=1, keepdims=True)

    def halves(width, d):
        cut = 256 if width > 256 else 128
        return (slice(None), pl.ds(0, cut) if d == 0 else pl.ds(cut, width - cut))

    def spread_index(s, p, off, core=None):
        order = ORDERS[s]
        fixed = {axis: here.pos[axis] for axis in order[p + 1 :]}
        fixed[order[p]] = here.coord(order[p], off)
        return (here.core if core is None else core,) + here.index(fixed)

    def spread(s, p, off, core=None):
        return held[s].at[spread_index(s, p, off, core)]

    def spread_half(s, p, off, d):
        width = held[s].shape[-1]
        return held[s].at[spread_index(s, p, off) + halves(width, d)]

    def direct_gather(s, p):
        return p == 0 or (p == 1 and s < 3) or (p == 2 and s >= 6)

    def near_gather(s, p, d, h, sending):
        axis = ORDERS[s][p]
        off = (1, 3)[d]
        ref = spread_half(s, p, 0 if sending else 4 - off, h)
        return remote(
            ref, ref, nsem.at[s, p, d, h, 0], nsem.at[s, p, d, h, 1], here.at(axis, off if sending else 4 - off)
        )

    def gather_near(s, p):
        axis = ORDERS[s][p]
        for h in range(2):
            for d in range(2):
                go(near_gather(s, p, d, (d + h) % 2, True))
        if direct_gather(s, p):
            ref = spread(s, p, 0)
            go(remote(ref, ref, fsem.at[s, p, 0, 0], fsem.at[s, p, 0, 1], here.at(axis, 2)))
        if p == 2:
            give(s, 0, 0)

    def gather_far(s, p):
        axis = ORDERS[s][p]
        for d, (off, back) in enumerate(((1, 3), (3, 1))):
            near_gather(s, p, d, d, False).wait_recv()
            if not direct_gather(s, p):
                ref = spread_half(s, p, back, d)
                go(remote(ref, ref, fsem.at[s, p, d, 0], fsem.at[s, p, d, 1], here.at(axis, off)))

    def gather_end(s, p):
        axis = ORDERS[s][p]
        for d, back in enumerate((3, 1)):
            near_gather(s, p, d, 1 - d, False).wait_recv()
            if p == 2:
                give(s, 1 + d, back)
        if direct_gather(s, p):
            ref = spread(s, p, 2)
            remote(ref, ref, fsem.at[s, p, 0, 0], fsem.at[s, p, 0, 1], here.at(axis, 2)).wait_recv()
        else:
            for d, back in enumerate((3, 1)):
                ref = spread_half(s, p, 2, d)
                remote(ref, ref, fsem.at[s, p, d, 0], fsem.at[s, p, d, 1], here.at(axis, back)).wait_recv()
        if p == 2:
            give(s, 3, 2)

    def give(s, k, off):
        ref = spread(s, 2, off)
        go(remote(ref, ref, csem.at[s, k, 0], csem.at[s, k, 1], here.at(flip=True)))

    def take(s):
        for k, off in enumerate((0, 3, 1, 2)):
            ref = spread(s, 2, off, 1 - here.core)
            remote(ref, ref, csem.at[s, k, 0], csem.at[s, k, 1], here.at(flip=True)).wait_recv()

    group = 32 * rows
    block = 16 * rows
    slots = 16 * CAP
    mine = (ep * 4 + z) // 2

    def rows_at(i):
        return pl.ds(pl.multiple_of(i * group, group), group)

    def span(s):
        return slice(STARTS[s], STARTS[s] + WIDTHS[s])

    def lane_of(value, wanted):
        lane = lax.broadcasted_iota(jnp.int32, value.shape, 1)
        return jnp.sum(jnp.where(wanted(lane), value, 0.0), axis=1, keepdims=True)

    def select():
        row = lax.broadcasted_iota(jnp.int32, (block, block), 0)
        col = lax.broadcasted_iota(jnp.int32, (block, block), 1)
        earlier = ((row // rows == col // rows) & (col < row)).astype(jnp.bfloat16)
        token = lax.broadcasted_iota(jnp.int32, (block, slots), 0)
        slot = lax.broadcasted_iota(jnp.int32, (block, slots), 1)
        near = token // rows == slot // CAP
        turn_of = lax.rem(slot, CAP).astype(jnp.float32)
        eye = (
            lax.broadcasted_iota(jnp.int32, (slots, slots), 0) == lax.broadcasted_iota(jnp.int32, (slots, slots), 1)
        ).astype(jnp.bfloat16)

        def one(i, carry):
            marks = held[0][i // 4, lax.rem(i, 4), :, :, :, WIDTHS[0] :].reshape(block, 128)
            rank = lane_of(
                jnp.dot(earlier, marks, preferred_element_type=jnp.float32), lambda lane: lane == mine
            )
            chosen = lane_of(marks.astype(jnp.float32), lambda lane: lane == mine)
            hit = jnp.where(near & (rank == turn_of), chosen, 0.0).astype(jnp.bfloat16)
            back[i] = hit
            sel[i] = lax.dot_general(
                eye, hit, (((1,), (1,)), ((), ())), preferred_element_type=jnp.float32
            ).astype(jnp.bfloat16)
            return carry

        lax.fori_loop(0, 8, one, 0)

    def tokens_of(s, i, cols):
        return held[s][i // 4, i % 4, :, :, :, cols].reshape(block, cols.stop - cols.start)

    def consume(s):
        if s == 0:
            select()
            loads[0].wait()
            loads[1].wait()
        width = WIDTHS[s]
        for i in range(8):
            chosen = jnp.dot(sel[i], tokens_of(s, i, slice(0, width)), preferred_element_type=jnp.float32)
            picked[slots * i : slots * i + slots, :width] = chosen.astype(jnp.bfloat16)
        for i in range(2):
            part = slice(4 * slots * i, 4 * slots * (i + 1))
            value = jnp.dot(picked[part, :width], gu[span(s), :], preferred_element_type=jnp.float32)
            total[part, :] = value if s == 0 else total[part, :] + value

    def start(s):
        place = (here.core, here.pos["y"], here.pos["x"], here.pos["z"], slice(None))
        held[s][place + (pl.ds(0, WIDTHS[s]),)] = own[:, columns(s)]
        if s == 0:
            held[s][place + (pl.ds(WIDTHS[s], 128),)] = own[:, pl.ds(D, 128)]
        if s == n - 1:
            held[s][place + (pl.ds(WIDTHS[s], 128),)] = own[:, pl.ds(D + 128, 128)]
        gather_near(s, 0)

    def second(s):
        gather_far(s, 0)
        gather_end(s, 0)
        gather_near(s, 1)

    def second_far(s):
        gather_far(s, 1)

    def third(s):
        gather_end(s, 1)
        gather_near(s, 2)

    def third_far(s):
        gather_far(s, 2)

    def last(s):
        gather_end(s, 2)

    def use(s):
        take(s)
        consume(s)

    def run(*steps):
        for phase, group_of in steps:
            for s in group_of:
                phase(s)

    squares, logits = [], []
    named = find()
    own[:, D : D + 128] = jnp.concatenate(
        [named.astype(jnp.float32), jnp.zeros((rows, 128 - experts), jnp.float32)], axis=1
    ).astype(jnp.bfloat16)
    for step in range(n + LAGS[-1]):
        for phase, lag in zip((phase0, phase1, phase2, phase3), LAGS):
            if 0 <= step - lag < n:
                phase(step - lag)
    for copy in early:
        copy.wait_send()
    scale = lax.rsqrt(jnp.maximum(sum(squares) / D, 0.25))
    probs = route(named, sum(logits) * scale)
    high = scale.astype(jnp.bfloat16)
    low = scale - high.astype(jnp.float32)
    lane = lax.broadcasted_iota(jnp.int32, (rows, 128 - experts), 1)
    tail = jnp.where(lane == 0, high.astype(jnp.float32), jnp.where(lane == 1, low, 0.0))
    own[:, D + 128 :] = jnp.concatenate([probs, tail], axis=1).astype(jnp.bfloat16)
    run(
        (start, (8,)), (second_far, (3, 4, 5)), (second, (6, 7, 8)), (third_far, (0, 1, 2)), (third, (3, 4, 5)),
        (second_far, (6, 7, 8)), (last, (0, 1, 2)),
    )
    for s in range(3):
        run((use, (s,)), (third_far, (3 + s,)), (third, (6 + s,)))
    run((last, (3, 4, 5)))
    for s in range(3, 6):
        run((use, (s,)), (third_far, (3 + s,)))
    run((last, (6, 7, 8)), (use, (6, 7, 8)))
    for copy in sends:
        copy.wait_send()
    sends.clear()
    loads[2].wait()
    for i in range(8):
        tail = tokens_of(n - 1, i, slice(WIDTHS[n - 1], WIDTHS[n - 1] + 128))
        tail = jnp.dot(sel[i], tail, preferred_element_type=jnp.float32)
        prob = lane_of(tail, lambda lane: lane == mine)
        factor = lane_of(tail, lambda lane: lane // 2 == experts // 2)
        part = slice(slots * i, slots * i + slots)
        gate_val = total[part, :hidden] * factor
        value = gate_val / (1.0 + jnp.exp(-gate_val)) * (total[part, hidden:] * factor) * prob
        act[block * i : block * i + block, :] = jnp.dot(
            back[i], value.astype(jnp.bfloat16), preferred_element_type=jnp.float32
        ).astype(jnp.bfloat16)

    def fold(s, p, off):
        order = ORDERS[s][::-1]
        fixed = {axis: here.pos[axis] for axis in order[:p]}
        fixed[order[p]] = here.coord(order[p], off)
        return here.index(fixed)

    def direct_fold(s, p):
        return p >= 1

    def merged(s, p, off):
        index = fold(s, p, off)
        if p == 0:
            mine = held[s][(here.core,) + index + (slice(None), pl.ds(0, WIDTHS[s]))]
            return mine + inner[s][index]
        return inner[s][index]

    def core_copy(s):
        return remote(
            held[s].at[1 - here.core, :, :, :, :, pl.ds(0, WIDTHS[s])],
            inner[s],
            rcore.at[s, 0],
            rcore.at[s, 1],
            here.at(flip=True),
        )

    def produce(s):
        def step(core):
            def one(h, carry):
                i = 2 * core + h
                value = jnp.dot(
                    act[rows_at(i), :], down[:, span(s)], preferred_element_type=jnp.float32
                )
                held[s][core, pl.ds(2 * h, 2), :, :, :, : WIDTHS[s]] = value.astype(jnp.bfloat16).reshape(
                    2, 4, 4, rows, WIDTHS[s]
                )
                return carry

            lax.fori_loop(0, 2, one, 0)

        step(1 - here.core)
        go(core_copy(s))
        step(here.core)

    def half_of(s, ref, index, d):
        return ref.at[index + halves(WIDTHS[s], d)]

    def lead(p):
        return (slice(None),) * (2 - p)

    def far_copy(s, p, d, sending):
        axis = ORDERS[s][2 - p]
        index = fold(s, p, 2)
        if direct_fold(s, p):
            return remote(
                inner[s].at[index], fars[s][p], rfar.at[s, p, 0, 0], rfar.at[s, p, 0, 1], here.at(axis, 2)
            )
        return remote(
            half_of(s, inner[s], index, d),
            half_of(s, fars[s][p], lead(p), d),
            rfar.at[s, p, d, 0],
            rfar.at[s, p, d, 1],
            here.at(axis, (1, 3)[d]),
        )

    def near_copy(s, p, d, h):
        axis = ORDERS[s][2 - p]
        off = (1, 3)[d]
        return remote(
            half_of(s, inner[s], fold(s, p, off), h),
            half_of(s, nears[s][p], (d,) + lead(p), h),
            rnear.at[s, p, d, h, 0],
            rnear.at[s, p, d, h, 1],
            here.at(axis, off),
        )

    def fold_far(s, p):
        if p == 0:
            core_copy(s).wait_recv()
            inner[s][fold(s, 0, 2)] = merged(s, 0, 2)
        for d in range(1 if direct_fold(s, p) else 2):
            go(far_copy(s, p, d, True))
        for d, off in enumerate((1, 3)):
            if p == 0:
                inner[s][fold(s, p, off)] = merged(s, p, off)
            go(near_copy(s, p, d, 1 - d))
            if direct_fold(s, p):
                go(near_copy(s, p, d, d))

    def fold_near(s, p):
        for d, off in enumerate((1, 3)):
            far_copy(s, p, d, False).wait_recv()
            part = fold(s, p, off) + halves(WIDTHS[s], d)
            inner[s][part] = inner[s][part] + fars[s][p][lead(p) + halves(WIDTHS[s], d)]
            go(near_copy(s, p, d, d))

    def fold_end(s, p):
        value = merged(s, p, 0).astype(jnp.float32)
        for d in range(2):
            for h in range(2):
                near_copy(s, p, d, h).wait_recv()
            value = value + nears[s][p][d].astype(jnp.float32)
        if direct_fold(s, p):
            far_copy(s, p, 0, False).wait_recv()
            value = value + fars[s][p][...].astype(jnp.float32)
        if p == 2:
            mixed[:, span(s)] = mixed[:, span(s)] + value
        else:
            inner[s][fold(s, p, 0)] = value.astype(jnp.bfloat16)

    def next_fold(s, p):
        fold_end(s, p - 1)
        fold_far(s, p)

    phases = (
        (produce, 0),
        (lambda s: fold_far(s, 0), 1),
        (lambda s: fold_near(s, 0), 3),
        (lambda s: next_fold(s, 1), 5),
        (lambda s: next_fold(s, 2), 7),
        (lambda s: fold_end(s, 2), 9),
    )
    for step in range(n + phases[-1][1]):
        for phase, lag in phases:
            if 0 <= step - lag < n:
                phase(step - lag)
    for copy in sends:
        copy.wait_send()


def run_layer(queries, new_keys, new_values, cache_keys, cache_values, cache_len, out_proj, resid, gain, router, ids,
              gate_slab, up_slab, down_slab):
    rows, width = resid.shape
    hidden = gate_slab.shape[2]
    n = len(ORDERS)
    dma, bf = pltpu.SemaphoreType.DMA, jnp.bfloat16
    vmem, anywhere = pl.BlockSpec(memory_space=pltpu.VMEM), pl.BlockSpec(memory_space=pl.ANY)
    extra = 128
    shapes = [
        pltpu.VMEM((rows, width + 2 * extra), bf),
        pltpu.VMEM((32, H // 32, rows, HD), bf),
        pltpu.VMEM(cache_keys.shape, bf),
        pltpu.VMEM(cache_values.shape, bf),
        pltpu.VMEM((H * rows, HD), jnp.float32),
        pltpu.VMEM((H * rows, HD), jnp.float32),
        pltpu.VMEM(new_keys.shape, jnp.float32),
        pltpu.VMEM(new_values.shape, jnp.float32),
        pltpu.VMEM(out_proj.shape, bf),
        pltpu.VMEM((32, H // 32, rows, HD), bf),
        pltpu.VMEM((3, 4, rows, width), bf),
        pltpu.VMEM((4, rows, width), bf),
        pltpu.VMEM((3, rows, width), bf),
        dma((3,)),
        dma((32, 2)),
        dma((n, 2)),
        dma((n, 4, 4, 2)),
        dma((n, 4, 2)),
        pltpu.VMEM((gate_slab.shape[1], 2 * hidden), bf),
        pltpu.VMEM(down_slab.shape[1:], bf),
        pltpu.VMEM((128 * rows, hidden), bf),
        pltpu.VMEM((128 * CAP, 2 * hidden), jnp.float32),
        pltpu.VMEM((128 * CAP, max(WIDTHS)), bf),
        pltpu.VMEM((8, 16 * CAP, 16 * rows), bf),
        pltpu.VMEM((8, 16 * rows, 16 * CAP), bf),
        dma((3,)),
        dma((n, 3, 2, 2, 2)),
        dma((n, 3, 2, 2)),
        dma((n, 4, 2)),
        dma((n, 3, 2, 2, 2)),
        dma((n, 3, 2, 2)),
        dma((n, 2)),
    ]
    shapes += [pltpu.VMEM((2, 4, 4, 4, rows, w + extra * (s in (0, n - 1))), bf) for s, w in enumerate(WIDTHS)]
    shapes += [pltpu.VMEM((4, 4, 4, rows, w), bf) for w in WIDTHS]
    shapes += [pltpu.VMEM((2,) + (4,) * (2 - p) + (rows, w), bf) for w in WIDTHS for p in range(3)]
    shapes += [pltpu.VMEM((4,) * (2 - p) + (rows, w), bf) for w in WIDTHS for p in range(3)]
    return pl.pallas_call(
        layer_kernel,
        out_shape=jax.ShapeDtypeStruct((rows, width), jnp.float32),
        in_specs=[vmem, vmem, vmem, anywhere, anywhere, pl.BlockSpec(memory_space=pltpu.SMEM), anywhere]
        + [vmem] * 4
        + [anywhere] * 3,
        out_specs=vmem,
        scratch_shapes=shapes,
        compiler_params=pltpu.CompilerParams(
            collective_id=0, has_side_effects=True, vmem_limit_bytes=VMEM_LIMIT
        ),
    )(
        queries, new_keys, new_values, cache_keys, cache_values, cache_len, out_proj, resid, gain, router, ids,
        gate_slab, up_slab, down_slab,
    )


def local(
    resid,
    queries,
    new_keys,
    new_values,
    cache_keys,
    cache_values,
    cache_len,
    out_proj,
    norm_gain,
    router,
    expert_ids,
    gate_slab,
    up_slab,
    down_slab,
):
    return run_layer(
        queries, new_keys, new_values, cache_keys, cache_values, cache_len, out_proj, resid,
        norm_gain.reshape(1, -1), router.T, expert_ids.T, gate_slab, up_slab, down_slab,
    )


def solution(mesh):
    in_specs = (
        P(("ep", "dp"), None),
        P(("ep", "dp"), None),
        P(("ep", "dp"), None),
        P(("ep", "dp"), None),
        P(("ep", "dp"), None, None),
        P(("ep", "dp"), None, None),
        P(("ep", "dp")),
        P("ep", None),
        P(),
        P(),
        P(("ep", "dp"), None),
        P(("ep", "dp"), None, None),
        P(("ep", "dp"), None, None),
        P(("ep", "dp"), None, None),
    )
    out_specs = P(("ep", "dp"), None)
    return jax.shard_map(local, mesh=mesh, in_specs=in_specs, out_specs=out_specs, check_vma=False)
```

time: 158 us -> 149 us (0.943)
  Pallas kernels: 156 us -> 147 us
  other arithmetic: 1.69 us -> 0 us
  local copies, waits for them, and re-layouts: 0.01 us -> 1.67 us
    pallas_call x2 -> x1, Pallas kernels: 156 us -> 147 us  [run_layer(): pl.pallas_call(layer_kernel, out_shape=jax.ShapeDtypeStruct((rows, width)...]
    add x1 -> x0, other arithmetic: 1.69 us -> none  [local(): return hidden + run_experts(packed, gate_slab, up_slab, down_slab)]
    unnamed x2 -> x1, local copies, waits for them, and re-layouts: 0.01 us -> 1.67 us
where the time goes in v3:
time: 149 us
  Pallas kernels  147 us (99%)
  local copies, waits for them, and re-layouts  1.67 us (1%)
    pallas_call x1, Pallas kernels, run_layer(): pl.pallas_call(layer_kernel, out_shape=jax.ShapeDtypeStruct((rows, width)...  147 us

profile of v3, /device:TPU:0, one launch (start us, length us, event | category | flops | bytes accessed | tf_op | source)
XLA Modules:
  0.0 148.5 jit_solution(12970399084157299416)
XLA Ops:
  0.0 146.9 %shard_map.136 = f32[16,4096]{1,0:T(8,128)} custom-call(bf16[16,8192]{1,0:T(8,128)(2,1)} %queries.1, bf16[16,512]{1,0:T(8,128)(2,1)} %new_keys.1, bf16[16,512]{1,0:T(8,128)(2,1)} %new_values.1, bf16[16,128,512]{2,1,0:T(8,128)(2,1)} %keys_hbm.1, bf16[16,128,512]{2,1,0:T(8,128)(2,1)} %values_hbm.1, s32[16]{0:T(128)} %lengths.1, bf16[256,4096]{1,0:T(8,128)(2,1)} %weight_hbm.1, ...), custom_call_target="tpu_custom_call" | custom-call | tf_op jit(solution)/shard_map/pallas_call | solution.py:658
  146.9 1.7 %copy.16 = f32[16,4096]{1,0:T(8,128)} copy(f32[16,4096]{1,0:T(8,128)} %shard_map.136) | data formatting | bytes 524288

commit v4 on v3

--- a/solution.py
+++ b/solution.py
@@ -78,11 +78,11 @@
         os[rows, :] = blended + own_weight * spread(nv[pl.ds(t, 1), :])
 
     def several(i, carry):
-        for k in range(4):
-            one(4 * i + k)
+        for k in range(8):
+            one(8 * i + k)
         return carry
 
-    lax.fori_loop(0, tokens // 4, several, 0)
+    lax.fori_loop(0, tokens // 8, several, 0)
     attended[...] = os[...].astype(jnp.bfloat16).reshape(attended.shape)
 
 

time: 149 us -> 148 us (level)
  no operation moved by 1% of the time
where the time goes in v4:
time: 148 us
  Pallas kernels  147 us (99%)
  local copies, waits for them, and re-layouts  1.67 us (1%)
    pallas_call x1, Pallas kernels, run_layer(): pl.pallas_call(layer_kernel, out_shape=jax.ShapeDtypeStruct((rows, width)...  147 us

profile of v4, /device:TPU:0, one launch (start us, length us, event | category | flops | bytes accessed | tf_op | source)
XLA Modules:
  0.0 148.2 jit_solution(14968301511637050831)
XLA Ops:
  0.0 146.5 %shard_map.136 = f32[16,4096]{1,0:T(8,128)} custom-call(bf16[16,8192]{1,0:T(8,128)(2,1)} %queries.1, bf16[16,512]{1,0:T(8,128)(2,1)} %new_keys.1, bf16[16,512]{1,0:T(8,128)(2,1)} %new_values.1, bf16[16,128,512]{2,1,0:T(8,128)(2,1)} %keys_hbm.1, bf16[16,128,512]{2,1,0:T(8,128)(2,1)} %values_hbm.1, s32[16]{0:T(128)} %lengths.1, bf16[256,4096]{1,0:T(8,128)(2,1)} %weight_hbm.1, ...), custom_call_target="tpu_custom_call" | custom-call | tf_op jit(solution)/shard_map/pallas_call | solution.py:658
  146.5 1.7 %copy.16 = f32[16,4096]{1,0:T(8,128)} copy(f32[16,4096]{1,0:T(8,128)} %shard_map.136) | data formatting | bytes 524288
